TPU v7x, 128 devices: a whole 4x4x4 slice. The times are simulated.
128 devices in a mesh: dp: 16 (over y, z_lo, core), tp: 8 (over x, z_hi).
Axes of the slice: x: 4, y: 4, z: 4 (z_hi: 2, z_lo: 2; z = z_hi * 2 + z_lo), core: 2. Of those that a mesh axis runs over, the one named last changes fastest.
Arguments:
- x_tokens: bfloat16 [16384, 8192], P(('dp', 'tp')), may hold values from -24 to 24
- segment_ids: int32 [16, 1024], P('dp'), may hold values from 0 to 3, never falling along the last dimension, each value on 1 to 512 neighbouring positions
- attended_grad: bfloat16 [16384, 4096], P('dp', 'tp'), may hold values from -6 to 6
- norm_gain: float32 [8192], replicated, may hold values from 0.1 to 1.9
- w_query: bfloat16 [8192, 4096], P(None, 'tp'), may hold values from -1 to 1
- w_key: bfloat16 [8192, 1024], P(None, 'tp'), may hold values from -4 to 4
- w_value: bfloat16 [8192, 1024], P(None, 'tp'), may hold values from -0.0625 to 0.0625
Outputs:
- attended: bfloat16 [16384, 4096], P('dp', 'tp')
- input_grad: bfloat16 [16384, 8192], P(('dp', 'tp'))
- gain_grad: float32 [8192], replicated
- grad_query: float32 [8192, 4096], P('dp', 'tp')
- grad_key: float32 [8192, 1024], P('dp', 'tp')
- grad_value: float32 [8192, 1024], P('dp', 'tp')
Inputs may be any that keep to these rules, and one draw needn't show every extreme that they name: `segment_ids`: along each replica's row the numbers never fall; every number 0 to 3 covers one run of 1 to 512 positions.
All inputs are finite; a program needn't handle non-finite values.
Results may differ from a plain program's by a relative error of at most 0.028.
The roundings to bfloat16 on the way count: a program that leaves them out, or rounds other values in their place, can miss the bound.
Values may be sent and summed in bfloat16 or wider, within the bound.
A program may use at most 256 MiB of HBM per device.

v0:
```python
import jax
import jax.numpy as jnp
from jax import lax
from jax.sharding import Mesh
from jax.sharding import PartitionSpec as P

HD = 128
TP = ("tp_0", "tp_1")
DP = ("dp_0", "dp_1", "dp_2")
DP_TP = ("dp_0", "dp_1", "dp_2", "tp_0", "tp_1")


epsilon = 1e-05
rope_base = 500000.0


def one_axis_at_a_time(array, axes):
    for axis in axes:
        array = lax.psum(array, axis)
    return array


def rope_tables(segment_row, head_dim):
    length = segment_row.shape[0]
    earlier = (segment_row[None, :] < segment_row[:, None]).astype(jnp.int32)
    offset = jnp.arange(length, dtype=jnp.int32) - jnp.sum(earlier, axis=1)
    half_dim = head_dim // 2
    inverse_freq = rope_base ** (-(jnp.arange(half_dim, dtype=jnp.float32) * 2.0 / head_dim))
    angle = offset.astype(jnp.float32)[:, None] * inverse_freq[None, :]
    return (jnp.cos(angle)[:, None, :], jnp.sin(angle)[:, None, :])


def attend_mask(segment_row):
    length = segment_row.shape[0]
    position = jnp.arange(length, dtype=jnp.int32)
    return (position[None, :] <= position[:, None]) & (segment_row[None, :] == segment_row[:, None])


def apply_rope(head_rows, cosine_table, sine_table, direction):
    half_dim = head_rows.shape[-1] // 2
    first_half = head_rows[..., :half_dim]
    second_half = head_rows[..., half_dim:]
    return jnp.concatenate(
        [
            first_half * cosine_table - direction * second_half * sine_table,
            second_half * cosine_table + direction * first_half * sine_table,
        ],
        axis=-1,
    )


def contract_first(left, right):
    return lax.dot_general(
        left, right, (((0,), (0,)), ((), ())), preferred_element_type=jnp.float32
    )


def contract_last(left, right):
    return lax.dot_general(
        left, right, (((1,), (1,)), ((), ())), preferred_element_type=jnp.float32
    )


def body(x_tokens, segment_ids, attended_grad, norm_gain, w_query, w_key, w_value):
    head_dim = HD
    q_heads = w_query.shape[1] // head_dim
    kv_heads = w_key.shape[1] // head_dim
    group = q_heads // kv_heads
    score_scale = float(head_dim) ** (-0.5)
    segment_row = segment_ids[0]
    as_float = x_tokens.astype(jnp.float32)
    inverse = lax.rsqrt(jnp.mean(as_float * as_float, axis=1, keepdims=True) + epsilon)
    x_hat = as_float * inverse
    normed = lax.all_gather((x_hat * norm_gain).astype(jnp.bfloat16), TP, axis=0, tiled=True)
    seq_len = normed.shape[0]
    cosine_table, sine_table = rope_tables(segment_row, head_dim)
    allowed = attend_mask(segment_row)
    query_f = jnp.dot(normed, w_query, preferred_element_type=jnp.float32).reshape(
        seq_len, q_heads, head_dim
    )
    queries = apply_rope(query_f, cosine_table, sine_table, 1.0).astype(jnp.bfloat16)
    key_f = jnp.dot(normed, w_key, preferred_element_type=jnp.float32).reshape(
        seq_len, kv_heads, head_dim
    )
    key_rows = apply_rope(key_f, cosine_table, sine_table, 1.0).astype(jnp.bfloat16)
    values_in = (
        jnp.dot(normed, w_value, preferred_element_type=jnp.float32)
        .astype(jnp.bfloat16)
        .reshape(seq_len, kv_heads, head_dim)
    )
    grouped = queries.reshape(seq_len, kv_heads, group, head_dim)
    out_grouped = attended_grad.reshape(seq_len, kv_heads, group, head_dim)
    block_rows = min(512, seq_len)
    block_count = seq_len // block_rows
    value_total = jnp.zeros((seq_len, kv_heads, head_dim), jnp.float32)
    key_total = jnp.zeros((seq_len, kv_heads, head_dim), jnp.float32)
    attended_parts = []
    query_parts = []
    for block_index in range(block_count):
        first = block_index * block_rows
        last = first + block_rows
        query_block = grouped[first:last]
        keys_seen = key_rows[:last]
        values_seen = values_in[:last]
        mask_block = allowed[first:last, :last]
        scores = (
            jnp.einsum("skgd,tkd->kgst", query_block, keys_seen, preferred_element_type=jnp.float32)
            * score_scale
        )
        scores = jnp.where(mask_block[None, None], scores, -1e30)
        highest = jnp.max(scores, axis=3, keepdims=True)
        exponent = jnp.exp(scores - highest)
        probability = exponent / jnp.sum(exponent, axis=3, keepdims=True)
        weights_b = probability.astype(jnp.bfloat16)
        attended_block = jnp.einsum(
            "kgst,tkd->skgd", weights_b, values_seen, preferred_element_type=jnp.float32
        ).astype(jnp.bfloat16)
        grad_block = out_grouped[first:last]
        row_delta = jnp.sum(
            grad_block.astype(jnp.float32) * attended_block.astype(jnp.float32), axis=3
        )
        value_part = jnp.einsum(
            "kgst,skgd->tkd", weights_b, grad_block, preferred_element_type=jnp.float32
        )
        prob_d = jnp.einsum(
            "skgd,tkd->kgst", grad_block, values_seen, preferred_element_type=jnp.float32
        )
        score_d = (
            probability * (prob_d - jnp.transpose(row_delta, (1, 2, 0))[..., None]) * score_scale
        ).astype(jnp.bfloat16)
        query_parts.append(
            jnp.einsum("kgst,tkd->skgd", score_d, keys_seen, preferred_element_type=jnp.float32)
        )
        key_part = jnp.einsum(
            "kgst,skgd->tkd", score_d, query_block, preferred_element_type=jnp.float32
        )
        padding = ((0, seq_len - last), (0, 0), (0, 0))
        value_total = value_total + jnp.pad(value_part, padding)
        key_total = key_total + jnp.pad(key_part, padding)
        attended_parts.append(attended_block)
    attended = jnp.concatenate(attended_parts, axis=0).reshape(seq_len, q_heads * head_dim)
    query_rot = jnp.concatenate(query_parts, axis=0).reshape(seq_len, q_heads, head_dim)
    query_d = (
        apply_rope(query_rot, cosine_table, sine_table, -1.0)
        .astype(jnp.bfloat16)
        .reshape(seq_len, q_heads * head_dim)
    )
    key_d = (
        apply_rope(key_total, cosine_table, sine_table, -1.0)
        .astype(jnp.bfloat16)
        .reshape(seq_len, kv_heads * head_dim)
    )
    value_flat = value_total.astype(jnp.bfloat16).reshape(seq_len, kv_heads * head_dim)
    total = contract_last(query_d, w_query)
    total = total + contract_last(key_d, w_key)
    normed_d = lax.psum_scatter(
        (total + contract_last(value_flat, w_value)).astype(jnp.bfloat16),
        TP,
        scatter_dimension=0,
        tiled=True,
    ).astype(jnp.float32)
    scaled_d = normed_d * norm_gain
    input_grad = (
        inverse * (scaled_d - x_hat * jnp.mean(scaled_d * x_hat, axis=1, keepdims=True))
    ).astype(jnp.bfloat16)
    gain_grad = one_axis_at_a_time(jnp.sum(normed_d * x_hat, axis=0), DP_TP)
    merged = lax.psum_scatter(
        jnp.concatenate(
            [
                contract_first(normed, query_d),
                contract_first(normed, key_d),
                contract_first(normed, value_flat),
            ],
            axis=1,
        ).astype(jnp.bfloat16),
        DP,
        scatter_dimension=0,
        tiled=True,
    ).astype(jnp.float32)
    query_cols = query_d.shape[1]
    key_cols = key_d.shape[1]
    grad_query = merged[:, :query_cols]
    grad_key = merged[:, query_cols : query_cols + key_cols]
    grad_value = merged[:, query_cols + key_cols :]
    return (attended, input_grad, gain_grad, grad_query, grad_key, grad_value)


def solution(mesh):
    torus = Mesh(mesh.devices.reshape(4, 2, 2, 4, 2), ("dp_0", "dp_1", "dp_2", "tp_0", "tp_1"))
    return jax.shard_map(
        body,
        mesh=torus,
        in_specs=(
            P(DP_TP, None),
            P(DP, None),
            P(DP, TP),
            P(),
            P(None, TP),
            P(None, TP),
            P(None, TP),
        ),
        out_specs=(P(DP, TP), P(DP_TP, None), P(), P(DP, TP), P(DP, TP), P(DP, TP)),
        check_vma=False,
    )
```

profile of v0, /device:TPU:1, one launch (start us, length us, event | category | flops | bytes accessed | tf_op | source)
XLA Modules:
  0.0 725.9 jit_solution(1995013405429331707)
XLA Ops:
  7.2 2.2 fusion.14
  9.5 0.5 copy-done.11
  10.0 3.5 fusion.12
  13.6 0.6 fusion.24
  14.2 0.7 slice.82
  14.9 2.1 fusion.114
  17.0 2.0 copy.86
  19.0 1.0 copy.87
  20.0 0.5 convert_reduce_fusion
  20.5 3.1 broadcast_multiply_fusion
  23.6 178.0 %all-gather.2.cloned.1.call-done = bf16[1024,8192]{1,0:T(8,128)(2,1)} async-done(((bf16[128,8192]{1,0:T(8,128)(2,1)}), bf16[1024,8192]{1,0:T(8,128)(2,1)}) %all-gather.2.cloned.1.call-update) | async-done | bytes 16777232 | tf_op jit(solution)/shard_map/all_gather | solution.py:74
  201.6 12.2 %convolution_bitcast_fusion.1 = f32[1024,1,128]{0,2,1:T(8,128)} fusion(bf16[1024,8192]{1,0:T(8,128)(2,1)} %all-gather.2.cloned.1.call-done, bf16[8192,128]{1,0:T(8,128)(2,1)S(1)} %copy-done), kind=kOutput, calls=%fused_computation.64 | convolution fusion | flops 2147483648 | bytes 19398656 | tf_op jit(solution)/shard_map/dot_general | solution.py:82
  213.8 2.1 fusion.84
  216.0 16.0 %fusion.116 = f32[1024,512]{0,1:T(8,128)} fusion(bf16[1024,8192]{1,0:T(8,128)(2,1)} %all-gather.2.cloned.1.call-done, bf16[8192,512]{1,0:T(8,128)(2,1)} %param.11), kind=kOutput, calls=%fused_computation.132 | convolution fusion | flops 8589934592 | bytes 27262976 | tf_op jit(solution)/shard_map/dot_general | solution.py:78
  232.0 3.1 fusion.113
  235.1 3.2 copy.85
  238.2 3.2 copy.84
  241.4 2.9 subtract_convert_fusion.1
  244.7 1.2 fusion.28
  245.9 0.9 fusion.27
  246.8 1.2 fusion.66
  248.0 0.5 slice-done.1
  248.5 1.1 slice-done.2
  249.6 1.2 slice-done.3
  250.8 0.6 copy-done.4
  251.4 4.5 convolution_convert_fusion.3
  255.9 2.3 fusion.73
  258.2 1.8 fusion.19
  259.9 1.2 fusion.69
  261.1 1.4 fusion.38
  262.5 1.7 fusion.5
  264.2 1.8 fusion.4
  266.1 3.4 fusion.72
  269.5 3.4 fusion.63
  272.9 3.3 fusion.16
  276.2 1.8 convolution_bitcast_fusion
  278.0 1.5 fusion.59
  279.5 1.3 fusion.97
  281.0 0.7 subtract_convert_fusion
  281.8 0.6 pad_maximum_fusion.2
  282.3 1.3 copy.51
  283.7 9.7 %convolution_convert_fusion.1 = bf16[8192,128]{0,1:T(8,128)(2,1)} fusion(bf16[1024,8192]{1,0:T(8,128)(2,1)} %all-gather.2.cloned.1.call-done, bf16[1024,128]{1,0:T(8,128)(2,1)} %fusion.63), kind=kOutput, calls=%fused_computation.3 | convolution fusion | flops 2148532224 | bytes 19136512 | tf_op jit(solution)/shard_map/dot_general | solution.py:53
  293.4 14.8 %convolution_convert_fusion = bf16[8192,512]{0,1:T(8,128)(2,1)} fusion(bf16[1024,512]{0,1:T(8,128)(2,1)} %bitcast.256, bf16[1024,8192]{1,0:T(8,128)(2,1)} %all-gather.2.cloned.1.call-done), kind=kOutput, calls=%fused_computation.2 | convolution fusion | flops 8594128896 | bytes 26214400 | tf_op jit(solution)/shard_map/dot_general | solution.py:53
  308.2 3.8 convolution_convert_fusion.2
  312.0 12.8 %pad_maximum_fusion = bf16[8192,768]{0,1:T(8,128)(2,1)} fusion(bf16[8192,128]{0,1:T(8,128)(2,1)} %convolution_convert_fusion.1, bf16[8192,128]{0,1:T(8,128)(2,1)} %convolution_convert_fusion.2, bf16[8192,512]{0,1:T(8,128)(2,1)S(1)} %copy-done.1), kind=kLoop, calls=%fused_computation.1 | loop fusion | flops 37748736 | bytes 25165824 | tf_op jit(solution)/shard_map/concatenate | solution.py:168
  324.8 13.9 %fusion.93 = f32[1024,8192]{1,0:T(8,128)} fusion(bf16[8192,128]{1,0:T(8,128)(2,1)S(1)} %copy-done, bf16[1024,64]{0,1:T(8,128)(2,1)S(1)} %get-tuple-element.31, bf16[1024,64]{0,1:T(8,128)(2,1)S(1)} %get-tuple-element.30), kind=kOutput, calls=%fused_computation.111 | convolution fusion | flops 2148007936 | bytes 35913728 | tf_op jit(solution)/shard_map/dot_general | solution.py:59
  338.7 19.1 %fusion.117 = f32[1024,8192]{1,0:T(8,128)} fusion(bf16[1024,512]{0,1:T(8,128)(2,1)S(1)} %bitcast.257, bf16[8192,512]{1,0:T(8,128)(2,1)} %param.11), kind=kOutput, calls=%fused_computation.133 | convolution fusion | flops 8589934592 | bytes 42991616 | tf_op jit(solution)/shard_map/dot_general | solution.py:59
  357.7 29.4 %add_convert_fusion = bf16[1024,8192]{1,0:T(8,128)(2,1)} fusion(f32[1024,8192]{1,0:T(8,128)} %fusion.117, f32[1024,8192]{1,0:T(8,128)} %fusion.93, bf16[1024,128]{1,0:T(8,128)(2,1)S(1)} %copy-done.9, bf16[8192,128]{1,0:T(8,128)(2,1)} %param.13), kind=kOutput, calls=%fused_computation | convolution fusion | flops 2172649472 | bytes 86245376 | tf_op jit(solution)/shard_map/dot_general | solution.py:59
  387.1 1.3 pad_maximum_fusion.1
  388.5 1.3 copy.58
  389.8 73.2 %reduce-scatter.5.cloned.1.call-done = bf16[512,768]{0,1:T(8,128)(2,1)} async-done(((bf16[8192,768]{0,1:T(8,128)(2,1)}), bf16[512,768]{0,1:T(8,128)(2,1)}) %reduce-scatter.5.cloned.1.call-update) | async-done | bytes 786448 | tf_op jit(solution)/shard_map/reduce_scatter | solution.py:167
  463.0 1.0 fusion.115
  464.1 0.8 copy.61
  464.9 0.8 copy.60
  465.7 1.2 slice.94
  466.9 1.3 copy.59
  468.2 189.2 %reduce-scatter.3.cloned.1.call-done = bf16[128,8192]{1,0:T(8,128)(2,1)} async-done(((bf16[1024,8192]{1,0:T(8,128)(2,1)}), bf16[128,8192]{1,0:T(8,128)(2,1)}) %reduce-scatter.3.cloned.1.call-update) | async-done | bytes 2097168 | tf_op jit(solution)/shard_map/reduce_scatter | solution.py:156
  657.4 3.7 fusion.15
  661.1 13.3 %psum.35 = f32[8192]{0:T(1024)S(1)} all-reduce(f32[8192]{0:T(1024)S(1)} %get-tuple-element.18), channel_id=1, replica_groups=mesh['dp_0'=4,'dp_1'=2,'dp_2'=2,'tp_0'=4,'tp_1'=2] {'dp_0'}, use_global_device_ids=true, to_apply=%region_11.12 | all-reduce | flops 8192 | bytes 65536 | tf_op jit(solution)/shard_map/psum | solution.py:19
  674.5 6.0 psum.36
  680.5 12.4 %psum.37 = f32[8192]{0:T(1024)S(1)} all-reduce(f32[8192]{0:T(1024)S(1)} %psum.36), channel_id=1, replica_groups=mesh['dp_0'=4,'dp_1'=2,'dp_2'=2,'tp_0'=4,'tp_1'=2] {'dp_2'}, use_global_device_ids=true, to_apply=%region_13.14 | all-reduce | flops 8192 | bytes 65536 | tf_op jit(solution)/shard_map/psum | solution.py:19
  692.9 11.7 %psum.38 = f32[8192]{0:T(1024)S(1)} all-reduce(f32[8192]{0:T(1024)S(1)} %psum.37), channel_id=1, replica_groups=mesh['dp_0'=4,'dp_1'=2,'dp_2'=2,'tp_0'=4,'tp_1'=2] {'tp_0'}, use_global_device_ids=true, to_apply=%region_14.15 | all-reduce | flops 8192 | bytes 65536 | tf_op jit(solution)/shard_map/psum | solution.py:19
  704.6 9.8 %psum.39 = f32[8192]{0:T(1024)} all-reduce(f32[8192]{0:T(1024)S(1)} %psum.38), channel_id=1, replica_groups=mesh['dp_0'=4,'dp_1'=2,'dp_2'=2,'tp_0'=4,'tp_1'=2] {'tp_1'}, use_global_device_ids=true, to_apply=%region_15.16 | all-reduce | flops 8192 | bytes 65536 | tf_op jit(solution)/shard_map/psum | solution.py:19
  714.4 4.6 fusion.11
  (52 shorter events, 0.8 us)
Async XLA Ops:
  7.2 194.4 %copy-start = (bf16[8192,128]{1,0:T(8,128)(2,1)S(1)}, bf16[8192,128]{1,0:T(8,128)(2,1)}, u32[]{:S(2)}) copy-start(bf16[8192,128]{1,0:T(8,128)(2,1)} %param.12) | copy-start | bytes 6291460
  7.2 6.4 copy-start.10
  7.2 194.4 %all-gather.2.cloned.1.call-start = ((), (), s32[]{:S(2)}) async-start(), calls=%async_computation.2 | async-start | bytes 18874368 | tf_op jit(solution)/shard_map/all_gather | solution.py:74
  9.5 0.5 copy-start.11
  13.5 449.5 %reduce-scatter.5.cloned.1.call-start = ((), (), s32[]{:S(2)}) async-start(), calls=%async_computation.4 | async-start | bytes 13369344 | tf_op jit(solution)/shard_map/reduce_scatter | solution.py:167
  241.4 3.2 copy-start.2
  244.6 2.1 copy-start.7
  244.6 3.4 slice-start
  245.9 2.6 slice-start.1
  246.8 2.8 slice-start.2
  246.8 4.0 slice-start.3
  246.8 4.6 copy-start.4
  264.2 1.9 copy-start.6
  278.0 3.0 copy-start.3
  283.7 24.5 %slice-start.4 = ((s8[16777216]{0:T(1024)(128)(4,1)}), s8[4194304]{0:T(1024)(128)(4,1)S(1)}, s32[]{:S(2)}) async-start(s8[16777216]{0:T(1024)(128)(4,1)} %bitcast.248), calls=%async_computation.9 | async-start | bytes 8388608
  283.7 24.5 %slice-start.5 = ((s8[16777216]{0:T(1024)(128)(4,1)}), s8[4194304]{0:T(1024)(128)(4,1)S(1)}, s32[]{:S(2)}) async-start(s8[16777216]{0:T(1024)(128)(4,1)} %bitcast.248), calls=%async_computation.10 | async-start | bytes 8388608
  293.4 14.8 %slice-start.6 = ((s8[16777216]{0:T(1024)(128)(4,1)}), s8[4194304]{0:T(1024)(128)(4,1)S(1)}, s32[]{:S(2)}) async-start(s8[16777216]{0:T(1024)(128)(4,1)} %bitcast.248), calls=%async_computation.11 | async-start | bytes 8388608
  293.4 14.8 %slice-start.7 = ((s8[16777216]{0:T(1024)(128)(4,1)}), s8[4194304]{0:T(1024)(128)(4,1)S(1)}, s32[]{:S(2)}) async-start(s8[16777216]{0:T(1024)(128)(4,1)} %bitcast.248), calls=%async_computation.12 | async-start | bytes 8388608
  308.2 3.8 copy-start.1
  324.8 13.9 %copy-start.5 = (bf16[1024,4,128]{0,2,1:T(8,128)(2,1)S(1)}, bf16[1024,4,128]{0,2,1:T(8,128)(2,1)}, u32[]{:S(2)}) copy-start(bf16[1024,4,128]{0,2,1:T(8,128)(2,1)} %copy.51) | copy-start | bytes 3145732
  324.8 332.6 %reduce-scatter.3.cloned.1.call-start = ((), (), s32[]{:S(2)}) async-start(), calls=%async_computation.3 | async-start | bytes 18874368 | tf_op jit(solution)/shard_map/reduce_scatter | solution.py:156
  338.7 19.1 %copy-start.9 = (bf16[1024,128]{1,0:T(8,128)(2,1)S(1)}, bf16[1024,128]{1,0:T(8,128)(2,1)}, u32[]{:S(2)}) copy-start(bf16[1024,128]{1,0:T(8,128)(2,1)} %fusion.63) | copy-start | bytes 786436
  388.5 268.9 %copy-start.8 = (f32[8192]{0:T(1024)S(1)}, f32[8192]{0:T(1024)}, u32[]{:S(2)}) copy-start(f32[8192]{0:T(1024)} %param.10) | copy-start | bytes 98308
  388.5 268.9 %copy-start.12 = (f32[128]{0:T(128)S(1)}, f32[128]{0:T(128)}, u32[]{:S(2)}) copy-start(f32[128]{0:T(128)} %copy-done.11) | copy-start | bytes 1540
Sparse Core Ops, SparseCore 0:
  13.6 187.9 all-gather.1
  324.9 138.1 reduce-scatter.4
  467.0 190.3 reduce-scatter.2
where the time goes:
time: 740 us; the launch traced here: 726 us
  waiting for transfers between devices  440 us (59%)
  matrix products  147 us (20%)
  blocking collectives  53.2 us (7%)
  other arithmetic  43.2 us (6%)
  local copies, waits for them, and re-layouts  27.1 us (4%)
  between operations  14.5 us (2%)
    reduce_scatter x1, waiting for transfers between devices, body(): lax.psum_scatter((total + contract_last(value_flat, w_value)).astype(jnp....  189 us
    all_gather x1, waiting for transfers between devices, body(): lax.all_gather((x_hat * norm_gain).astype(jnp.bfloat16), TP, axis=0, tile...  178 us
    reduce_scatter x1, waiting for transfers between devices, body(): lax.psum_scatter(jnp.concatenate([contract_first(normed, query_d), contra...  73.2 us
    dot_general x3, matrix products, contract_last(): lax.dot_general(left, right, (((1,), (1,)), ((), ())), preferred_element_...  62.3 us
    psum x5, blocking collectives, one_axis_at_a_time(): array = lax.psum(array, axis)  53.2 us
    dot_general x3, matrix products, contract_first(): lax.dot_general(left, right, (((0,), (0,)), ((), ())), preferred_element_...  28.3 us
    unnamed x50, local copies, waits for them, and re-layouts  17.6 us
    dot_general x1, matrix products, body(): jnp.dot(normed, w_query, preferred_element_type=jnp.float32)  16 us
  transfers between devices with their start and end apart: 3, of which 3 were waited for; matrix products, arithmetic and copies ran while one was open for 11% of the time, Pallas kernels for 0%

commit v1 on v0

v1 whole, which is shorter than its diff:
```python
import jax
import jax.numpy as jnp
from jax import lax
from jax.experimental import pallas as pl
from jax.experimental.pallas import tpu as pltpu
from jax.sharding import Mesh
from jax.sharding import PartitionSpec as P

HD = 128
SPLIT = 4608
MESH = pl.DeviceIdType.MESH
TP = ("x", "zh")
DP = ("y", "zl", "c")
DP_TP = ("y", "zl", "c", "x", "zh")
epsilon = 1e-05
rope_base = 500000.0
def gather_kernel(n_ref, wq_ref, wk_ref, wv_ref, qkv_ref, full_ref, a_s, w_s, send, recv, local):
    x=lax.axis_index("x"); z=lax.axis_index("zh")
    right=lax.rem(x+1,4); left=lax.rem(x+3,4); far=lax.rem(x+2,4)
    to_right={"x":right}; to_left={"x":left}; to_z={"zh":1-z}
    half=a_s.shape[2]; rows=2*half
    lo=pl.ds(0,SPLIT); hi=pl.ds(SPLIT,a_s.shape[3]-SPLIT); every=pl.ds(0,a_s.shape[3])
    own=pltpu.make_async_copy(n_ref,a_s.at[2*x+z],local.at[0]); own.start()
    bar=pltpu.get_barrier_semaphore()
    for dev in (to_right,to_left,to_z):
        pl.semaphore_signal(bar,inc=1,device_id=dev,device_id_type=MESH)
    own.wait()
    pl.semaphore_wait(bar,3)
    wide=wq_ref.shape[1]; narrow=wk_ref.shape[1]
    loads=[pltpu.make_async_copy(wq_ref,w_s.at[:,pl.ds(0,wide)],local.at[1]),
           pltpu.make_async_copy(wk_ref,w_s.at[:,pl.ds(wide,narrow)],local.at[2]),
           pltpu.make_async_copy(wv_ref,w_s.at[:,pl.ds(wide+narrow,narrow)],local.at[3])]
    sent=[]
    def copy(k,sx,sz,h,cols,dev):
        ref=a_s.at[2*sx+sz,h,:,cols]
        return pltpu.make_async_remote_copy(src_ref=ref,dst_ref=ref,send_sem=send.at[k],recv_sem=recv.at[k],device_id=dev,device_id_type=MESH)
    def go(k,sx,sz,h,cols,dev):
        c=copy(k,sx,sz,h,cols,dev); c.start(); sent.append(c)
    def got(k,sx,sz,h,cols):
        copy(k,sx,sz,h,cols,to_z).wait_recv()
    o=1-z
    go(0,x,z,0,every,to_right); go(1,x,z,1,every,to_left)
    go(6,x,z,0,lo,to_z); go(7,x,z,1,lo,to_z)
    go(2,x,z,1,every,to_right); go(3,x,z,0,every,to_left)
    go(8,x,z,0,hi,to_z); go(9,x,z,1,hi,to_z)
    for c in loads: c.start()
    outs=[]
    def done(i,sx,sz):
        c=pltpu.make_async_copy(a_s.at[2*sx+sz],full_ref.at[2*sx+sz],local.at[4+i]); c.start(); outs.append(c)
    def project(slots):
        def one(i,_):
            s=slots(i)
            r=pl.ds(pl.multiple_of(s*rows,rows),rows)
            def part(j,_):
                kk=pl.ds(pl.multiple_of(j*KC,KC),KC)
                p=lax.dot_general(a_s[s,:,:,kk].reshape(rows,KC),w_s[kk,:],(((1,),(0,)),((),())),preferred_element_type=jnp.float32)
                qkv_ref[r,:]=jnp.where(j==0,p,qkv_ref[r,:]+p)
                return 0
            lax.fori_loop(0,a_s.shape[3]//KC,part,0)
            return 0
        return one
    KC=2048
    def run(n,f): lax.fori_loop(0,n,project(f),0)
    done(0,x,z)
    for c in loads: c.wait()
    run(1,lambda i: 2*x+z)
    got(0,left,z,0,every); go(4,left,z,0,every,to_right); go(10,left,z,0,hi,to_z)
    got(1,right,z,1,every); go(5,right,z,1,every,to_left); go(11,right,z,1,hi,to_z)
    got(6,x,o,0,lo); go(12,x,o,0,lo,to_right); got(7,x,o,1,lo); go(13,x,o,1,lo,to_left)
    go(14,x,o,1,lo,to_right); go(15,x,o,0,lo,to_left)
    got(2,left,z,1,every); go(16,left,z,1,hi,to_z)
    got(3,right,z,0,every); go(17,right,z,0,hi,to_z)
    done(1,left,z); done(2,right,z)
    got(8,x,o,0,hi); got(9,x,o,1,hi); done(3,x,o)
    run(2,lambda i: 2*lax.rem(x+1+2*i,4)+z)
    got(4,far,z,0,every); go(18,far,z,0,hi,to_z)
    got(5,far,z,1,every); go(19,far,z,1,hi,to_z)
    done(4,far,z)
    run(1,lambda i: 2*x+o)
    got(12,left,o,0,lo); go(20,left,o,0,lo,to_right)
    got(13,right,o,1,lo); go(21,right,o,1,lo,to_left)
    run(1,lambda i: 2*far+z)
    got(10,left,o,0,hi); got(11,right,o,1,hi)
    got(14,left,o,1,lo); got(16,left,o,1,hi); done(5,left,o)
    got(15,right,o,0,lo); got(17,right,o,0,hi); done(6,right,o)
    run(2,lambda i: 2*lax.rem(x+1+2*i,4)+o)
    got(20,far,o,0,lo); got(21,far,o,1,lo); got(18,far,o,0,hi); got(19,far,o,1,hi); done(7,far,o)
    run(1,lambda i: 2*far+o)
    for c in sent: c.wait_send()
    for c in outs: c.wait()

def gather_project(normed,wq,wk,wv):
    rows,feat=normed.shape
    cols=wq.shape[1]+2*wk.shape[1]
    any_=pl.BlockSpec(memory_space=pl.ANY); vm=pl.BlockSpec(memory_space=pltpu.VMEM)
    qkv,full=pl.pallas_call(gather_kernel,
        out_shape=(jax.ShapeDtypeStruct((8*rows,cols),jnp.float32),jax.ShapeDtypeStruct((8,2,rows//2,feat),jnp.bfloat16)),
        in_specs=[any_]*4,out_specs=(vm,any_),
        scratch_shapes=[pltpu.VMEM((8,2,rows//2,feat),jnp.bfloat16),pltpu.VMEM((feat,cols),jnp.bfloat16),
            pltpu.SemaphoreType.DMA((22,)),pltpu.SemaphoreType.DMA((22,)),pltpu.SemaphoreType.DMA((12,))],
        compiler_params=pltpu.CompilerParams(collective_id=1,has_side_effects=True,vmem_limit_bytes=60*2**20),name="gather_project",
        cost_estimate=pl.CostEstimate(flops=2*8*rows*feat*cols,bytes_accessed=48*2**20,transcendentals=0),
    )(normed.reshape(2,rows//2,feat),wq,wk,wv)
    return qkv,full.reshape(8*rows,feat)
BQ=256
def _nt(a,b): return lax.dot_general(a,b,(((1,),(1,)),((),())),preferred_element_type=jnp.float32)
def _tn(a,b): return lax.dot_general(a,b,(((0,),(0,)),((),())),preferred_element_type=jnp.float32)
def _nn(a,b): return lax.dot_general(a,b,(((1,),(0,)),((),())),preferred_element_type=jnp.float32)

def attention_kernel(qkv_ref, go_ref, cos_ref, sin_ref, segr_ref, segc_ref, att_ref, d_ref, q_s, k_s, v_s, dk_s, dv_s):
    seq=qkv_ref.shape[0]; heads=go_ref.shape[1]//HD; width=heads*HD
    scale=float(HD)**-0.5
    def rope(u,c,s): return u*c+pltpu.roll(u,HD//2,1)*s
    nb=seq//BQ
    for b in range(nb):
        r=slice(b*BQ,(b+1)*BQ)
        c=cos_ref[r,:]; s=sin_ref[r,:]
        for h in range(heads):
            q_s[r,h*HD:(h+1)*HD]=rope(qkv_ref[r,h*HD:(h+1)*HD],c,s).astype(jnp.bfloat16)
        k_s[r,:]=rope(qkv_ref[r,width:width+HD],c,s).astype(jnp.bfloat16)
        v_s[r,:]=qkv_ref[r,width+HD:width+2*HD].astype(jnp.bfloat16)
    dk_s[...]=jnp.zeros_like(dk_s)
    dv_s[...]=jnp.zeros_like(dv_s)
    for b in range(nb):
        r=slice(b*BQ,(b+1)*BQ)
        lo=max(0,(b*BQ-511)//BQ*BQ); hi=(b+1)*BQ
        kr=slice(lo,hi)
        rows=lax.broadcasted_iota(jnp.int32,(BQ,hi-lo),0)+b*BQ
        cols=lax.broadcasted_iota(jnp.int32,(BQ,hi-lo),1)+lo
        mask=(cols<=rows)&(segr_ref[0:1,kr]==segc_ref[r,0:1])
        def head(h,_):
            hs=pl.ds(pl.multiple_of(h*HD,HD),HD)
            q=q_s[r,hs]; go=go_ref[r,hs]
            k=k_s[kr,:]; v=v_s[kr,:]
            sc=jnp.where(mask,_nt(q,k)*scale,-1e30)
            m=jnp.max(sc,axis=1,keepdims=True)
            e=jnp.exp(sc-m)
            p=e*(1.0/jnp.sum(e,axis=1,keepdims=True))
            w=p.astype(jnp.bfloat16)
            o=_nn(w,v).astype(jnp.bfloat16)
            att_ref[r,hs]=o
            delta=jnp.sum(go.astype(jnp.float32)*o.astype(jnp.float32),axis=1,keepdims=True)
            dv_s[kr,:]+=_tn(w,go)
            dp=_nt(go,v)
            ds=(p*(dp-delta)*scale).astype(jnp.bfloat16)
            dq=_nn(ds,k)
            d_ref[r,hs]=rope(dq,cos_ref[r,:],-sin_ref[r,:]).astype(jnp.bfloat16)
            dk_s[kr,:]+=_tn(ds,q)
            return 0
        lax.fori_loop(0,heads,head,0,unroll=True)
    d_ref[:,width:width+HD]=rope(dk_s[...],cos_ref[...],-sin_ref[...]).astype(jnp.bfloat16)
    d_ref[:,width+HD:width+2*HD]=dv_s[...].astype(jnp.bfloat16)

def attention(qkv,go,cos,sin,segs):
    seq=qkv.shape[0]
    vm=pl.BlockSpec(memory_space=pltpu.VMEM)
    return pl.pallas_call(attention_kernel,
        out_shape=(jax.ShapeDtypeStruct(go.shape,jnp.bfloat16),jax.ShapeDtypeStruct(qkv.shape,jnp.bfloat16)),
        in_specs=[vm]*6,out_specs=(vm,vm),
        scratch_shapes=[pltpu.VMEM(go.shape,jnp.bfloat16),pltpu.VMEM((seq,HD),jnp.bfloat16),pltpu.VMEM((seq,HD),jnp.bfloat16),pltpu.VMEM((seq,HD),jnp.float32),pltpu.VMEM((seq,HD),jnp.float32)],
        compiler_params=pltpu.CompilerParams(vmem_limit_bytes=60*2**20),name="attention",
        cost_estimate=pl.CostEstimate(flops=12*go.shape[1]*seq*seq//2,bytes_accessed=12*2**20,transcendentals=0),
    )(qkv,go,cos,sin,segs.reshape(1,seq),segs.reshape(seq,1))
CC=512
def scatter_kernel(d_ref, wq_ref, wk_ref, wv_ref, out_ref, w_s, po, pw, ro, rw, rq, rp, send, recv, local):
    x=lax.axis_index("x"); z=lax.axis_index("zh"); o=1-z
    right=lax.rem(x+1,4); left=lax.rem(x+3,4); far=lax.rem(x+2,4)
    to_right={"x":right}; to_left={"x":left}; to_z={"zh":o}
    feat=po.shape[3]; half=po.shape[2]; rows=2*half
    lo=pl.ds(0,SPLIT); hi=pl.ds(SPLIT,feat-SPLIT); every=pl.ds(0,feat)
    wide=wq_ref.shape[1]; narrow=wk_ref.shape[1]
    loads=[pltpu.make_async_copy(wq_ref,w_s.at[:,pl.ds(0,wide)],local.at[0]),
           pltpu.make_async_copy(wk_ref,w_s.at[:,pl.ds(wide,narrow)],local.at[1]),
           pltpu.make_async_copy(wv_ref,w_s.at[:,pl.ds(wide+narrow,narrow)],local.at[2])]
    for c in loads: c.start()
    bar=pltpu.get_barrier_semaphore()
    for dev in (to_right,to_left,to_z):
        pl.semaphore_signal(bar,inc=1,device_id=dev,device_id_type=MESH)
    for c in loads: c.wait()
    sent=[]
    f32=jnp.float32; bf=jnp.bfloat16
    def piece(sx,sz,j):
        cc=pl.ds(pl.multiple_of(j*CC,CC),CC)
        return cc,lax.dot_general(d_ref[2*sx+sz],w_s[cc,:],(((1,),(1,)),((),())),preferred_element_type=f32).reshape(2,half,CC)
    def compute_other(sx):
        def step(j,_):
            cc,p=piece(sx,o,j); po[sx,:,:,cc]=p.astype(bf); return 0
        lax.fori_loop(0,feat//CC,step,0)
    def compute_own(sx):
        def step(j,_):
            cc,p=piece(sx,z,j); pw[sx,:,:,cc]=p.astype(bf); return 0
        lax.fori_loop(0,SPLIT//CC,step,0)
        got(12+0,sx)
        def step2(j,_):
            cc,p=piece(sx,z,j)
            qq=pl.ds(pl.multiple_of(j*CC-SPLIT,CC),CC)
            pw[sx,:,:,cc]=(p+rq[sx,:,:,qq].astype(f32)).astype(bf); return 0
        lax.fori_loop(SPLIT//CC,feat//CC,step2,0)
    def copy(k,src,dst,dev):
        return pltpu.make_async_remote_copy(src_ref=src,dst_ref=dst,send_sem=send.at[k],recv_sem=recv.at[k],device_id=dev,device_id_type=MESH)
    def go(k,src,dst,dev):
        c=copy(k,src,dst,dev); c.start(); sent.append(c)
    qsem={}
    def got(k,sx=None):
        if k==12:
            copy(12+sx,rq.at[sx],rq.at[sx],to_z).wait_recv()
        elif k<6: copy(k,ro.at[k],ro.at[k],to_z).wait_recv()
        elif k<12: copy(k,rw.at[k-6],rw.at[k-6],to_z).wait_recv()
        else: copy(k,rp.at[k-16],rp.at[k-16],to_z).wait_recv()
    def zsend(sx):
        go(12+sx,po.at[sx,:,:,hi],rq.at[sx],to_z)
    W=1024
    def add(dst,terms,width):
        def step(j,_):
            cc=pl.ds(pl.multiple_of(j*CC,CC),CC)
            acc=terms[0][:,cc].astype(f32)
            for t in terms[1:]: acc=acc+t[:,cc].astype(f32)
            dst[:,cc]=acc.astype(bf); return 0
        lax.fori_loop(0,width//CC,step,0)
    compute_other(far)
    pl.semaphore_wait(bar,3)
    go(0,po.at[far,0,:,lo],ro.at[0],to_right); go(1,po.at[far,1,:,lo],ro.at[1],to_left); zsend(far)
    compute_other(right); go(2,po.at[right,1,:,lo],ro.at[2],to_right); zsend(right)
    compute_other(left); go(3,po.at[left,0,:,lo],ro.at[3],to_left); zsend(left)
    compute_other(x); zsend(x)
    got(0); add(po.at[right,0],[po.at[right,0],ro.at[0]],SPLIT); go(4,po.at[right,0,:,lo],ro.at[4],to_right)
    got(1); add(po.at[left,1],[po.at[left,1],ro.at[1]],SPLIT); go(5,po.at[left,1,:,lo],ro.at[5],to_left)
    compute_own(far)
    go(6,pw.at[far,0],rw.at[0],to_right); go(7,pw.at[far,1],rw.at[1],to_left)
    got(3); got(4); add(po.at[x,0],[po.at[x,0],ro.at[4],ro.at[3]],SPLIT); go(16,po.at[x,0,:,lo],rp.at[0],to_z)
    got(2); got(5); add(po.at[x,1],[po.at[x,1],ro.at[5],ro.at[2]],SPLIT); go(17,po.at[x,1,:,lo],rp.at[1],to_z)
    compute_own(right); go(8,pw.at[right,1],rw.at[2],to_right)
    compute_own(left); go(9,pw.at[left,0],rw.at[3],to_left)
    got(6); add(pw.at[right,0],[pw.at[right,0],rw.at[0]],feat); go(10,pw.at[right,0],rw.at[4],to_right)
    got(7); add(pw.at[left,1],[pw.at[left,1],rw.at[1]],feat); go(11,pw.at[left,1],rw.at[5],to_left)
    compute_own(x)
    def final(h,a,b):
        def low(j,_):
            cc=pl.ds(pl.multiple_of(j*CC,CC),CC)
            out_ref[h,:,cc]=(pw[x,h,:,cc].astype(f32)+rw[a,:,cc].astype(f32)+rw[b,:,cc].astype(f32)+rp[h,:,cc].astype(f32)).astype(bf); return 0
        def high(j,_):
            cc=pl.ds(pl.multiple_of(j*CC,CC),CC)
            out_ref[h,:,cc]=(pw[x,h,:,cc].astype(f32)+rw[a,:,cc].astype(f32)+rw[b,:,cc].astype(f32)).astype(bf); return 0
        lax.fori_loop(0,SPLIT//CC,low,0)
        lax.fori_loop(SPLIT//CC,feat//CC,high,0)
    got(9); got(10); got(16); final(0,4,3)
    got(8); got(11); got(17); final(1,5,2)
    for c in sent: c.wait_send()

def project_scatter(d,wq,wk,wv):
    seq,cols=d.shape; feat=wq.shape[0]; rows=seq//8; half=rows//2
    any_=pl.BlockSpec(memory_space=pl.ANY); vm=pl.BlockSpec(memory_space=pltpu.VMEM)
    bf=jnp.bfloat16
    out=pl.pallas_call(scatter_kernel,
        out_shape=jax.ShapeDtypeStruct((2,half,feat),bf),
        in_specs=[vm]+[any_]*3,out_specs=vm,
        scratch_shapes=[pltpu.VMEM((feat,cols),bf),pltpu.VMEM((4,2,half,feat),bf),pltpu.VMEM((4,2,half,feat),bf),
            pltpu.VMEM((6,half,SPLIT),bf),pltpu.VMEM((6,half,feat),bf),pltpu.VMEM((4,2,half,feat-SPLIT),bf),pltpu.VMEM((2,half,SPLIT),bf),
            pltpu.SemaphoreType.DMA((18,)),pltpu.SemaphoreType.DMA((18,)),pltpu.SemaphoreType.DMA((3,))],
        compiler_params=pltpu.CompilerParams(collective_id=2,has_side_effects=True,vmem_limit_bytes=60*2**20),name="project_scatter",
        cost_estimate=pl.CostEstimate(flops=2*seq*feat*cols,bytes_accessed=32*2**20,transcendentals=0),
    )(d.reshape(8,rows,cols),wq,wk,wv)
    return out.reshape(rows,feat)

STAGES = ((("c",), (2,)), (("zl", "zh"), (2, 2)), (("y",), (4,)), (("x",), (4,)))


def place(axes, sizes, index):
    where = {}
    for axis, size in zip(reversed(axes), reversed(sizes)):
        where[axis] = lax.rem(index, size)
        index = lax.div(index, size)
    return where


def total_kernel(part_ref, out_ref, b0, b1, b2, b3, send, recv):
    bufs = (b0, b1, b2, b3)
    bar = pltpu.get_barrier_semaphore()
    plan = []
    for axes, sizes in STAGES:
        n = 1
        me = jnp.int32(0)
        for axis, size in zip(axes, sizes):
            n *= size
            me = me * size + lax.axis_index(axis)
        others = [lax.rem(me + k, n) for k in range(1, n)]
        plan.append((n, me, others, [place(axes, sizes, other) for other in others]))
    count = 0
    for n, me, others, devices in plan:
        for device in devices:
            pl.semaphore_signal(bar, inc=1, device_id=device, device_id_type=MESH)
            count += 1
    value = part_ref[...]
    pl.semaphore_wait(bar, count)
    for stage, (n, me, others, devices) in enumerate(plan):
        buf = bufs[stage]
        buf[me] = value
        copies = []
        for k, device in enumerate(devices):
            copy = pltpu.make_async_remote_copy(
                src_ref=buf.at[me],
                dst_ref=buf.at[me],
                send_sem=send.at[stage, k],
                recv_sem=recv.at[stage, me],
                device_id=device,
                device_id_type=MESH,
            )
            copy.start()
            copies.append(copy)
        for k, other in enumerate(others):
            pltpu.make_async_remote_copy(
                src_ref=buf.at[other],
                dst_ref=buf.at[other],
                send_sem=send.at[stage, k],
                recv_sem=recv.at[stage, other],
                device_id=devices[k],
                device_id_type=MESH,
            ).wait_recv()
        value = buf[0]
        for k in range(1, n):
            value = value + buf[k]
        for copy in copies:
            copy.wait_send()
    out_ref[...] = value


def total_over_devices(part):
    vm = pl.BlockSpec(memory_space=pltpu.VMEM)
    shape = (part.shape[0] // 128, 128)
    out = pl.pallas_call(
        total_kernel,
        out_shape=jax.ShapeDtypeStruct(shape, jnp.float32),
        in_specs=[vm],
        out_specs=vm,
        scratch_shapes=[
            pltpu.VMEM((2,) + shape, jnp.float32),
            pltpu.VMEM((4,) + shape, jnp.float32),
            pltpu.VMEM((4,) + shape, jnp.float32),
            pltpu.VMEM((4,) + shape, jnp.float32),
            pltpu.SemaphoreType.DMA((4, 4)),
            pltpu.SemaphoreType.DMA((4, 4)),
        ],
        compiler_params=pltpu.CompilerParams(collective_id=3, has_side_effects=True),
        name="total",
        cost_estimate=pl.CostEstimate(flops=10**9, bytes_accessed=10**6, transcendentals=0),
    )(part.reshape(shape))
    return out.reshape(part.shape)


def rope_tables(segment_row):
    length = segment_row.shape[0]
    earlier = (segment_row[None, :] < segment_row[:, None]).astype(jnp.int32)
    offset = jnp.arange(length, dtype=jnp.int32) - jnp.sum(earlier, axis=1)
    half_dim = HD // 2
    inverse_freq = rope_base ** (-(jnp.arange(half_dim, dtype=jnp.float32) * 2.0 / HD))
    angle = offset.astype(jnp.float32)[:, None] * inverse_freq[None, :]
    cosine, sine = jnp.cos(angle), jnp.sin(angle)
    return jnp.concatenate([cosine, cosine], axis=1), jnp.concatenate([-sine, sine], axis=1)


def body(x_tokens, segment_ids, attended_grad, norm_gain, w_query, w_key, w_value):
    segment_row = segment_ids[0]
    as_float = x_tokens.astype(jnp.float32)
    inverse = lax.rsqrt(jnp.mean(as_float * as_float, axis=1, keepdims=True) + epsilon)
    own = (as_float * inverse * norm_gain).astype(jnp.bfloat16)
    qkv, normed = gather_project(own, w_query, w_key, w_value)
    cosine, sine = rope_tables(segment_row)
    attended, heads_d = attention(qkv, attended_grad, cosine, sine, segment_row)
    products = lax.dot_general(
        normed, heads_d, (((0,), (0,)), ((), ())), preferred_element_type=jnp.float32
    ).astype(jnp.bfloat16)
    heads_d, products = lax.optimization_barrier((heads_d, products))
    merged = lax.psum_scatter(products, DP, scatter_dimension=0, tiled=True).astype(jnp.float32)
    normed_d = project_scatter(heads_d, w_query, w_key, w_value).astype(jnp.float32)
    x_hat = x_tokens.astype(jnp.float32) * inverse
    scaled_d = normed_d * norm_gain
    input_grad = (
        inverse * (scaled_d - x_hat * jnp.mean(scaled_d * x_hat, axis=1, keepdims=True))
    ).astype(jnp.bfloat16)
    gain_grad = total_over_devices(jnp.sum(normed_d * x_hat, axis=0))
    query_cols, key_cols = w_query.shape[1], w_key.shape[1]
    return (
        attended,
        input_grad,
        gain_grad,
        merged[:, :query_cols],
        merged[:, query_cols : query_cols + key_cols],
        merged[:, query_cols + key_cols :],
    )


def solution(mesh):
    torus = Mesh(mesh.devices.reshape(4, 2, 2, 4, 2), DP_TP)
    return jax.shard_map(
        body,
        mesh=torus,
        in_specs=(
            P(DP_TP, None),
            P(DP, None),
            P(DP, TP),
            P(),
            P(None, TP),
            P(None, TP),
            P(None, TP),
        ),
        out_specs=(P(DP, TP), P(DP_TP, None), P(), P(DP, TP), P(DP, TP), P(DP, TP)),
        check_vma=False,
    )
```

time: 740 us -> 444 us (0.60); the launches traced: 726 us -> 442 us
  waiting for transfers between devices: 440 us -> 0.02 us
  Pallas kernels: 0 us -> 385 us
  matrix products: 147 us -> 20.2 us
  blocking collectives: 53.2 us -> 0 us
  other arithmetic: 43.2 us -> 16.4 us
  local copies, waits for them, and re-layouts: 27.1 us -> 6.3 us
    pallas_call x0 -> x4, Pallas kernels: none -> 385 us  [the longest x1 230 us: project_scatter(): pl.pallas_call(scatter_kernel, out_shape=jax.ShapeDtypeStruct((2, half, f...]
    reduce_scatter x2 -> x1, waiting for transfers between devices: 262 us -> 0.01 us  [body(): lax.psum_scatter(products, DP, scatter_dimension=0, tiled=True)]
    all_gather x1 -> x0, waiting for transfers between devices: 178 us -> none  [body(): lax.all_gather((x_hat * norm_gain).astype(jnp.bfloat16), TP, axis=0, tile...]
    dot_general x21 -> x1, matrix products: 147 us -> 20.2 us  [body(): lax.dot_general(normed, heads_d, (((0,), (0,)), ((), ())), preferred_elem...]
    psum x5 -> x0, blocking collectives: 53.2 us -> none  [one_axis_at_a_time(): array = lax.psum(array, axis)]
    unnamed x50 -> x7, local copies, waits for them, and re-layouts: 17.6 us -> 0.63 us
    concatenate x5 -> x1, other arithmetic: 16.3 us -> 1.3 us  [rope_tables(): jnp.concatenate([cosine, cosine], axis=1)]
  transfers between devices with their start and end apart: 3 -> 1, of which waited for: 3 -> 0; matrix products, arithmetic and copies ran while one was open for 11% -> 2% of each run, Pallas kernels for 0% -> 56%
where the time goes in v1:
time: 444 us; the launch traced here: 442 us
  Pallas kernels  385 us (87%)
  matrix products  20.2 us (5%)
  other arithmetic  16.4 us (4%)
  between operations  14.1 us (3%)
  local copies, waits for them, and re-layouts  6.3 us (1%)
    pallas_call x1, Pallas kernels, project_scatter(): pl.pallas_call(scatter_kernel, out_shape=jax.ShapeDtypeStruct((2, half, f...  230 us
    pallas_call x1, Pallas kernels, gather_project(): pl.pallas_call(gather_kernel, out_shape=(jax.ShapeDtypeStruct((8 * rows,...  117 us
    dot_general x1, matrix products, body(): lax.dot_general(normed, heads_d, (((0,), (0,)), ((), ())), preferred_elem...  20.2 us
    pallas_call x1, Pallas kernels, attention(): pl.pallas_call(attention_kernel, out_shape=(jax.ShapeDtypeStruct(go.shape...  19.4 us
    pallas_call x1, Pallas kernels, total_over_devices(): pl.pallas_call(total_kernel, out_shape=jax.ShapeDtypeStruct(shape, jnp.fl...  18.9 us
  transfers between devices with their start and end apart: 1, of which 0 were waited for; matrix products, arithmetic and copies ran while one was open for 2% of the time, Pallas kernels for 56%

profile of v1, /device:TPU:1, one launch (start us, length us, event | category | flops | bytes accessed | tf_op | source)
XLA Modules:
  0.0 442.4 jit_solution(14578507375244765486)
XLA Ops:
  7.2 0.0 copy-start
  7.2 0.0 copy-start.1
  7.2 0.0 reduce-scatter.2.cloned.1.call-start
  7.2 2.2 fusion.8
  9.5 1.3 convert_reduce_fusion
  10.8 1.7 copy.14.segc_ref
  12.5 1.9 fusion.10
  14.4 0.0 copy-done
  14.5 0.0 copy-done.1
  14.5 1.9 fusion.6
  16.4 1.3 pad_maximum_fusion
  17.7 117.1 %gather_project.1 = (f32[1024,768]{1,0:T(8,128)}, bf16[8,2,64,8192]{3,2,1,0:T(8,128)(2,1)}) custom-call(bf16[2,64,8192]{2,1,0:T(8,128)(2,1)} %bitcast.14, bf16[8192,512]{1,0:T(8,128)(2,1)} %wq_ref.3, bf16[8192,128]{1,0:T(8,128)(2,1)} %wk_ref.3, bf16[8192,128]{1,0:T(8,128)(2,1)} %wv_ref.3), custom_call_target="tpu_custom_call" | custom-call | flops 12884901888 | bytes 50331648 | tf_op jit(solution)/shard_map/gather_project/pallas_call | solution.py:96
  134.7 19.4 %attention.1 = (bf16[1024,512]{1,0:T(8,128)(2,1)}, bf16[1024,768]{1,0:T(8,128)(2,1)}) custom-call(f32[1024,768]{1,0:T(8,128)} %get-tuple-element.12.qkv_ref, bf16[1024,512]{1,0:T(8,128)(2,1)} %go_ref.1, f32[1024,128]{1,0:T(8,128)} %get-tuple-element.25.cos_ref, f32[1024,128]{1,0:T(8,128)} %get-tuple-element.26.sin_ref, s32[1,1024]{1,0:T(1,128)} %segr_ref.1, ...), custom_call_target="tpu_custom_call" | custom-call | flops 3221225472 | bytes 12582912 | tf_op jit(solution)/shard_map/attention/pallas_call | solution.py:157
  154.1 20.2 %convolution_convert_fusion = bf16[8192,768]{1,0:T(8,128)(2,1)} fusion(bf16[1024,8192]{1,0:T(8,128)(2,1)} %bitcast.19, bf16[1024,768]{1,0:T(8,128)(2,1)} %get-tuple-element.16), kind=kOutput, calls=%fused_computation | convolution fusion | flops 12891193344 | bytes 30932992 | tf_op jit(solution)/shard_map/dot_general | solution.py:369
  174.3 0.0 reduce-scatter.2.cloned.1.call-update
  174.3 230.1 %project_scatter.1 = bf16[2,64,8192]{2,1,0:T(8,128)(2,1)} custom-call(bf16[8,128,768]{2,1,0:T(8,128)(2,1)} %bitcast.20, bf16[8192,512]{1,0:T(8,128)(2,1)} %wq_ref.3, bf16[8192,128]{1,0:T(8,128)(2,1)} %wk_ref.3, bf16[8192,128]{1,0:T(8,128)(2,1)} %wv_ref.3), custom_call_target="tpu_custom_call" | custom-call | flops 12884901888 | bytes 33554432 | tf_op jit(solution)/shard_map/project_scatter/pallas_call | solution.py:254
  404.4 3.7 fusion.9
  408.1 18.9 %total.1 = f32[64,128]{1,0:T(8,128)} custom-call(f32[64,128]{1,0:T(8,128)} %bitcast.17), custom_call_target="tpu_custom_call" | custom-call | flops 1000000000 | bytes 1000000 | tf_op jit(solution)/shard_map/total/pallas_call | solution.py:330
  427.0 0.0 copy-start.2
  427.0 4.0 fusion.5
  431.0 0.0 reduce-scatter.2.cloned.1.call-done
  431.0 1.8 fusion.11
  432.8 2.1 slice.12
  435.0 0.0 copy-done.2
  435.0 0.6 copy.16
  (4 shorter events, 0.0 us)
Async XLA Ops:
  7.2 7.3 %copy-start = (bf16[128,8192]{1,0:T(8,128)(2,1)S(1)}, bf16[128,8192]{1,0:T(8,128)(2,1)}, u32[]{:S(2)}) copy-start(bf16[128,8192]{1,0:T(8,128)(2,1)} %param.7) | copy-start | bytes 6291460
  7.2 7.3 %copy-start.1 = (f32[8192]{0:T(1024)S(1)}, f32[8192]{0:T(1024)}, u32[]{:S(2)}) copy-start(f32[8192]{0:T(1024)} %param.10) | copy-start | bytes 98308
  7.2 423.8 %reduce-scatter.2.cloned.1.call-start = ((), (), s32[]{:S(2)}) async-start(), calls=%async_computation.1 | async-start | bytes 13369344 | tf_op jit(solution)/shard_map/reduce_scatter | solution.py:373
  427.0 7.9 %copy-start.2 = (f32[64,128]{1,0:T(8,128)S(1)}, f32[64,128]{1,0:T(8,128)}, u32[]{:S(2)}) copy-start(f32[64,128]{1,0:T(8,128)} %total.1) | copy-start | bytes 98308
Sparse Core Ops, SparseCore 0:
  174.4 242.3 reduce-scatter.1

commit v2 on v1

--- a/solution.py
+++ b/solution.py
@@ -347,6 +347,90 @@
     return out.reshape(part.shape)
 
 
+def gradient_kernel(n_ref, d_ref, out_ref, n_s, dt_s, mine, theirs, send, recv, local):
+    c = lax.axis_index("c")
+    count = out_ref.shape[0]
+    width = out_ref.shape[2]
+
+    def load(i):
+        block = jnp.where(i < count, 2 * i + 1 - c, 2 * (i - count) + c)
+        cols = pl.ds(pl.multiple_of(block * width, width), width)
+        return pltpu.make_async_copy(n_ref.at[:, cols], n_s.at[i], local.at[i])
+
+    def start(i, _):
+        load(i).start()
+        return 0
+
+    lax.fori_loop(0, 2 * count, start, 0)
+    bar = pltpu.get_barrier_semaphore()
+    pl.semaphore_signal(bar, inc=1, device_id={"c": 1 - c}, device_id_type=MESH)
+    dt_s[...] = d_ref[...].T
+    pl.semaphore_wait(bar, 1)
+
+    def copy(i):
+        return pltpu.make_async_remote_copy(
+            src_ref=mine.at[i],
+            dst_ref=theirs.at[i],
+            send_sem=send.at[i],
+            recv_sem=recv.at[i],
+            device_id={"c": 1 - c},
+            device_id_type=MESH,
+        )
+
+    def product(i):
+        load(i).wait()
+        return jnp.dot(dt_s[...], n_s[i], preferred_element_type=jnp.float32)
+
+    def first(i, _):
+        mine[i] = product(i).astype(jnp.bfloat16)
+        copy(i).start()
+        return 0
+
+    def second(i, _):
+        part = product(i + count)
+        copy(i).wait_recv()
+        out_ref[i] = (part + theirs[i].astype(jnp.float32)).astype(jnp.bfloat16)
+        return 0
+
+    def last(i, _):
+        copy(i).wait_send()
+        return 0
+
+    lax.fori_loop(0, count, first, 0)
+    lax.fori_loop(0, count, second, 0)
+    lax.fori_loop(0, count, last, 0)
+
+
+def pair_gradient(normed, heads_d):
+    seq, feat = normed.shape
+    cols = heads_d.shape[1]
+    count, width = 8, feat // 16
+    vm = pl.BlockSpec(memory_space=pltpu.VMEM)
+    bf = jnp.bfloat16
+    return pl.pallas_call(
+        gradient_kernel,
+        out_shape=jax.ShapeDtypeStruct((count, cols, width), bf),
+        in_specs=[pl.BlockSpec(memory_space=pl.ANY), vm],
+        out_specs=vm,
+        scratch_shapes=[
+            pltpu.VMEM((2 * count, seq, width), bf),
+            pltpu.VMEM((cols, seq), bf),
+            pltpu.VMEM((count, cols, width), bf),
+            pltpu.VMEM((count, cols, width), bf),
+            pltpu.SemaphoreType.DMA((count,)),
+            pltpu.SemaphoreType.DMA((count,)),
+            pltpu.SemaphoreType.DMA((2 * count,)),
+        ],
+        compiler_params=pltpu.CompilerParams(
+            collective_id=4, has_side_effects=True, vmem_limit_bytes=60 * 2**20
+        ),
+        name="pair_gradient",
+        cost_estimate=pl.CostEstimate(
+            flops=2 * seq * feat * cols, bytes_accessed=32 * 2**20, transcendentals=0
+        ),
+    )(normed, heads_d)
+
+
 def rope_tables(segment_row):
     length = segment_row.shape[0]
     earlier = (segment_row[None, :] < segment_row[:, None]).astype(jnp.int32)
@@ -366,12 +450,14 @@
     qkv, normed = gather_project(own, w_query, w_key, w_value)
     cosine, sine = rope_tables(segment_row)
     attended, heads_d = attention(qkv, attended_grad, cosine, sine, segment_row)
-    products = lax.dot_general(
-        normed, heads_d, (((0,), (0,)), ((), ())), preferred_element_type=jnp.float32
-    ).astype(jnp.bfloat16)
+    products = pair_gradient(normed, heads_d)
     heads_d, products = lax.optimization_barrier((heads_d, products))
-    merged = lax.psum_scatter(products, DP, scatter_dimension=0, tiled=True).astype(jnp.float32)
-    normed_d = project_scatter(heads_d, w_query, w_key, w_value).astype(jnp.float32)
+    merged = lax.psum_scatter(products, "y", scatter_dimension=0, tiled=True)
+    normed_d = project_scatter(heads_d, w_query, w_key, w_value)
+    merged, normed_d = lax.optimization_barrier((merged, normed_d))
+    merged = lax.psum_scatter(merged, "zl", scatter_dimension=0, tiled=True)
+    merged = merged[0].T.astype(jnp.float32)
+    normed_d = normed_d.astype(jnp.float32)
     x_hat = x_tokens.astype(jnp.float32) * inverse
     scaled_d = normed_d * norm_gain
     input_grad = (

time: 444 us -> 344 us (0.77)
  Pallas kernels: 385 us -> 301 us
  matrix products: 20.2 us -> 0 us
  waiting for transfers between devices: 0.02 us -> 5.26 us
    pallas_call x1, Pallas kernels: 230 us -> 121 us  [project_scatter(): pl.pallas_call(scatter_kernel, out_shape=jax.ShapeDtypeStruct((2, half, f...]
    pallas_call x0 -> x1, Pallas kernels: none -> 23 us  [pair_gradient(): pl.pallas_call(gradient_kernel, out_shape=jax.ShapeDtypeStruct((count, co...]
    dot_general x1 -> x0, matrix products: 20.2 us -> none  [body(): lax.dot_general(normed, heads_d, (((0,), (0,)), ((), ())), preferred_elem...]
    reduce_scatter x1 -> x2, waiting for transfers between devices: 0.01 us -> 5.22 us  [the longest x1 5.2 us: body(): merged = lax.psum_scatter(merged, 'zl', scatter_dimension=0, tiled=True)]
  transfers between devices with their start and end apart: 1 -> 2, of which waited for: 0 -> 1; matrix products, arithmetic and copies ran while one was open for 2% -> 2% of each run, Pallas kernels for 56% -> 41%
where the time goes in v2:
time: 344 us; the launch traced here: 343 us
  Pallas kernels  301 us (88%)
  other arithmetic  17.8 us (5%)
  between operations  14.2 us (4%)
  local copies, waits for them, and re-layouts  5.44 us (2%)
  waiting for transfers between devices  5.26 us (2%)
    pallas_call x1, Pallas kernels, project_scatter(): pl.pallas_call(scatter_kernel, out_shape=jax.ShapeDtypeStruct((2, half, f...  121 us
    pallas_call x1, Pallas kernels, gather_project(): pl.pallas_call(gather_kernel, out_shape=(jax.ShapeDtypeStruct((8 * rows,...  117 us
    pallas_call x1, Pallas kernels, pair_gradient(): pl.pallas_call(gradient_kernel, out_shape=jax.ShapeDtypeStruct((count, co...  23 us
    pallas_call x1, Pallas kernels, total_over_devices(): pl.pallas_call(total_kernel, out_shape=jax.ShapeDtypeStruct(shape, jnp.fl...  20.3 us
    pallas_call x1, Pallas kernels, attention(): pl.pallas_call(attention_kernel, out_shape=(jax.ShapeDtypeStruct(go.shape...  19.4 us
  transfers between devices with their start and end apart: 2, of which 1 were waited for; matrix products, arithmetic and copies ran while one was open for 2% of the time, Pallas kernels for 41%

profile of v2, /device:TPU:1, one launch (start us, length us, event | category | flops | bytes accessed | tf_op | source)
XLA Modules:
  0.0 343.4 jit_solution(13054040584541948257)
XLA Ops:
  7.2 0.0 copy-start
  7.2 0.0 copy-start.1
  7.2 0.0 reduce-scatter.3.cloned.1.call-start
  7.2 2.2 fusion.8
  9.5 1.3 convert_reduce_fusion
  10.8 1.7 copy.20.segc_ref
  12.5 1.9 fusion.10
  14.4 0.0 copy-done
  14.5 0.0 copy-done.1
  14.5 1.9 fusion.6
  16.4 1.3 pad_maximum_fusion
  17.7 117.1 %gather_project.1 = (f32[1024,768]{1,0:T(8,128)}, bf16[8,2,64,8192]{3,2,1,0:T(8,128)(2,1)}) custom-call(bf16[2,64,8192]{2,1,0:T(8,128)(2,1)} %bitcast.15, bf16[8192,512]{1,0:T(8,128)(2,1)} %wq_ref.3, bf16[8192,128]{1,0:T(8,128)(2,1)} %wk_ref.3, bf16[8192,128]{1,0:T(8,128)(2,1)} %wv_ref.3), custom_call_target="tpu_custom_call" | custom-call | flops 12884901888 | bytes 50331648 | tf_op jit(solution)/shard_map/gather_project/pallas_call | solution.py:96
  134.7 19.4 %attention.1 = (bf16[1024,512]{1,0:T(8,128)(2,1)}, bf16[1024,768]{1,0:T(8,128)(2,1)}) custom-call(f32[1024,768]{1,0:T(8,128)} %get-tuple-element.14.qkv_ref, bf16[1024,512]{1,0:T(8,128)(2,1)} %go_ref.1, f32[1024,128]{1,0:T(8,128)} %get-tuple-element.47.cos_ref, f32[1024,128]{1,0:T(8,128)} %get-tuple-element.48.sin_ref, s32[1,1024]{1,0:T(1,128)} %segr_ref.1, ...), custom_call_target="tpu_custom_call" | custom-call | flops 3221225472 | bytes 12582912 | tf_op jit(solution)/shard_map/attention/pallas_call | solution.py:157
  154.1 23.0 %pair_gradient.1 = bf16[8,768,512]{2,1,0:T(8,128)(2,1)} custom-call(bf16[1024,8192]{1,0:T(8,128)(2,1)} %bitcast.20, bf16[1024,768]{1,0:T(8,128)(2,1)} %get-tuple-element.19.d_ref), custom_call_target="tpu_custom_call" | custom-call | flops 12884901888 | bytes 33554432 | tf_op jit(solution)/shard_map/pair_gradient/pallas_call | solution.py:410
  177.1 0.0 reduce-scatter.3.cloned.1.call-update
  177.1 0.0 reduce-scatter.5.cloned.1.call-start
  177.2 121.0 %project_scatter.1 = bf16[2,64,8192]{2,1,0:T(8,128)(2,1)} custom-call(bf16[8,128,768]{2,1,0:T(8,128)(2,1)} %bitcast.21, bf16[8192,512]{1,0:T(8,128)(2,1)} %wq_ref.3, bf16[8192,128]{1,0:T(8,128)(2,1)} %wk_ref.3, bf16[8192,128]{1,0:T(8,128)(2,1)} %wv_ref.3), custom_call_target="tpu_custom_call" | custom-call | flops 12884901888 | bytes 33554432 | tf_op jit(solution)/shard_map/project_scatter/pallas_call | solution.py:254
  298.2 0.0 reduce-scatter.3.cloned.1.call-done
  298.2 0.0 reduce-scatter.5.cloned.1.call-update
  298.2 3.7 %fusion.9 = (f32[8192]{0:T(1024)}, f32[128]{0:T(128)S(1)}) fusion(bf16[128,8192]{1,0:T(8,128)(2,1)S(1)} %copy-done, bf16[128,8192]{1,0:T(8,128)(2,1)} %bitcast.13, f32[128]{0:T(128)S(1)} %add_rsqrt_fusion, f32[8192]{0:T(1024)S(1)} %copy-done.1), kind=kLoop, calls=%fused_computation.13 | loop fusion | flops 8380288 | bytes 4260864 | tf_op jit(solution)/shard_map/reduce_sum | solution.py:466
  301.9 20.3 %total.1 = f32[64,128]{1,0:T(8,128)} custom-call(f32[64,128]{1,0:T(8,128)} %bitcast.18), custom_call_target="tpu_custom_call" | custom-call | flops 1000000000 | bytes 1000000 | tf_op jit(solution)/shard_map/total/pallas_call | solution.py:330
  322.2 4.0 %fusion.5 = bf16[128,8192]{1,0:T(8,128)(2,1)} fusion(bf16[128,8192]{1,0:T(8,128)(2,1)} %bitcast.14, bf16[128,8192]{1,0:T(8,128)(2,1)S(1)} %copy-done, f32[128]{0:T(128)S(1)} %broadcast_multiply_fusion, f32[8192]{0:T(1024)S(1)} %copy-done.1, f32[128]{0:T(128)S(1)} %add_rsqrt_fusion), kind=kLoop, calls=%fused_computation.9 | loop fusion | flops 8388608 | bytes 6325248 | tf_op jit(solution)/shard_map/convert_element_type | solution.py:465
  326.3 0.0 copy-start.2
  326.3 5.2 %reduce-scatter.5.cloned.1.call-done = bf16[1,768,512]{2,1,0:T(8,128)(2,1)} async-done(((bf16[2,768,512]{2,1,0:T(8,128)(2,1)}), bf16[1,768,512]{2,1,0:T(8,128)(2,1)}) %reduce-scatter.5.cloned.1.call-update) | async-done | bytes 786448 | tf_op jit(solution)/shard_map/reduce_scatter | solution.py:458
  331.5 1.3 convert_bitcast_fusion
  332.9 0.1 slice.12
  332.9 1.3 copy.21
  334.3 0.8 copy.23
  335.1 0.8 copy.22
  335.9 0.0 copy-done.2
  335.9 0.6 copy.25
  (5 shorter events, 0.1 us)
Async XLA Ops:
  7.2 7.3 %copy-start = (bf16[128,8192]{1,0:T(8,128)(2,1)S(1)}, bf16[128,8192]{1,0:T(8,128)(2,1)}, u32[]{:S(2)}) copy-start(bf16[128,8192]{1,0:T(8,128)(2,1)} %param.7) | copy-start | bytes 6291460
  7.2 7.3 %copy-start.1 = (f32[8192]{0:T(1024)S(1)}, f32[8192]{0:T(1024)}, u32[]{:S(2)}) copy-start(f32[8192]{0:T(1024)} %param.10) | copy-start | bytes 98308
  7.2 291.0 %reduce-scatter.3.cloned.1.call-start = ((), (), s32[]{:S(2)}) async-start(), calls=%async_computation.2 | async-start | bytes 7864320 | tf_op jit(solution)/shard_map/reduce_scatter | solution.py:455
  177.1 154.4 %reduce-scatter.5.cloned.1.call-start = ((), (), s32[]{:S(2)}) async-start(), calls=%async_computation.3 | async-start | bytes 2359296 | tf_op jit(solution)/shard_map/reduce_scatter | solution.py:458
  326.3 9.7 %copy-start.2 = (f32[64,128]{1,0:T(8,128)S(1)}, f32[64,128]{1,0:T(8,128)}, u32[]{:S(2)}) copy-start(f32[64,128]{1,0:T(8,128)} %total.1) | copy-start | bytes 98308
Sparse Core Ops, SparseCore 0:
  177.2 63.2 reduce-scatter.2
  298.3 33.1 reduce-scatter.4

commit v3 on v1

--- a/solution.py
+++ b/solution.py
@@ -161,108 +161,11 @@
         compiler_params=pltpu.CompilerParams(vmem_limit_bytes=60*2**20),name="attention",
         cost_estimate=pl.CostEstimate(flops=12*go.shape[1]*seq*seq//2,bytes_accessed=12*2**20,transcendentals=0),
     )(qkv,go,cos,sin,segs.reshape(1,seq),segs.reshape(seq,1))
-CC=512
-def scatter_kernel(d_ref, wq_ref, wk_ref, wv_ref, out_ref, w_s, po, pw, ro, rw, rq, rp, send, recv, local):
-    x=lax.axis_index("x"); z=lax.axis_index("zh"); o=1-z
-    right=lax.rem(x+1,4); left=lax.rem(x+3,4); far=lax.rem(x+2,4)
-    to_right={"x":right}; to_left={"x":left}; to_z={"zh":o}
-    feat=po.shape[3]; half=po.shape[2]; rows=2*half
-    lo=pl.ds(0,SPLIT); hi=pl.ds(SPLIT,feat-SPLIT); every=pl.ds(0,feat)
-    wide=wq_ref.shape[1]; narrow=wk_ref.shape[1]
-    loads=[pltpu.make_async_copy(wq_ref,w_s.at[:,pl.ds(0,wide)],local.at[0]),
-           pltpu.make_async_copy(wk_ref,w_s.at[:,pl.ds(wide,narrow)],local.at[1]),
-           pltpu.make_async_copy(wv_ref,w_s.at[:,pl.ds(wide+narrow,narrow)],local.at[2])]
-    for c in loads: c.start()
-    bar=pltpu.get_barrier_semaphore()
-    for dev in (to_right,to_left,to_z):
-        pl.semaphore_signal(bar,inc=1,device_id=dev,device_id_type=MESH)
-    for c in loads: c.wait()
-    sent=[]
-    f32=jnp.float32; bf=jnp.bfloat16
-    def piece(sx,sz,j):
-        cc=pl.ds(pl.multiple_of(j*CC,CC),CC)
-        return cc,lax.dot_general(d_ref[2*sx+sz],w_s[cc,:],(((1,),(1,)),((),())),preferred_element_type=f32).reshape(2,half,CC)
-    def compute_other(sx):
-        def step(j,_):
-            cc,p=piece(sx,o,j); po[sx,:,:,cc]=p.astype(bf); return 0
-        lax.fori_loop(0,feat//CC,step,0)
-    def compute_own(sx):
-        def step(j,_):
-            cc,p=piece(sx,z,j); pw[sx,:,:,cc]=p.astype(bf); return 0
-        lax.fori_loop(0,SPLIT//CC,step,0)
-        got(12+0,sx)
-        def step2(j,_):
-            cc,p=piece(sx,z,j)
-            qq=pl.ds(pl.multiple_of(j*CC-SPLIT,CC),CC)
-            pw[sx,:,:,cc]=(p+rq[sx,:,:,qq].astype(f32)).astype(bf); return 0
-        lax.fori_loop(SPLIT//CC,feat//CC,step2,0)
-    def copy(k,src,dst,dev):
-        return pltpu.make_async_remote_copy(src_ref=src,dst_ref=dst,send_sem=send.at[k],recv_sem=recv.at[k],device_id=dev,device_id_type=MESH)
-    def go(k,src,dst,dev):
-        c=copy(k,src,dst,dev); c.start(); sent.append(c)
-    qsem={}
-    def got(k,sx=None):
-        if k==12:
-            copy(12+sx,rq.at[sx],rq.at[sx],to_z).wait_recv()
-        elif k<6: copy(k,ro.at[k],ro.at[k],to_z).wait_recv()
-        elif k<12: copy(k,rw.at[k-6],rw.at[k-6],to_z).wait_recv()
-        else: copy(k,rp.at[k-16],rp.at[k-16],to_z).wait_recv()
-    def zsend(sx):
-        go(12+sx,po.at[sx,:,:,hi],rq.at[sx],to_z)
-    W=1024
-    def add(dst,terms,width):
-        def step(j,_):
-            cc=pl.ds(pl.multiple_of(j*CC,CC),CC)
-            acc=terms[0][:,cc].astype(f32)
-            for t in terms[1:]: acc=acc+t[:,cc].astype(f32)
-            dst[:,cc]=acc.astype(bf); return 0
-        lax.fori_loop(0,width//CC,step,0)
-    compute_other(far)
-    pl.semaphore_wait(bar,3)
-    go(0,po.at[far,0,:,lo],ro.at[0],to_right); go(1,po.at[far,1,:,lo],ro.at[1],to_left); zsend(far)
-    compute_other(right); go(2,po.at[right,1,:,lo],ro.at[2],to_right); zsend(right)
-    compute_other(left); go(3,po.at[left,0,:,lo],ro.at[3],to_left); zsend(left)
-    compute_other(x); zsend(x)
-    got(0); add(po.at[right,0],[po.at[right,0],ro.at[0]],SPLIT); go(4,po.at[right,0,:,lo],ro.at[4],to_right)
-    got(1); add(po.at[left,1],[po.at[left,1],ro.at[1]],SPLIT); go(5,po.at[left,1,:,lo],ro.at[5],to_left)
-    compute_own(far)
-    go(6,pw.at[far,0],rw.at[0],to_right); go(7,pw.at[far,1],rw.at[1],to_left)
-    got(3); got(4); add(po.at[x,0],[po.at[x,0],ro.at[4],ro.at[3]],SPLIT); go(16,po.at[x,0,:,lo],rp.at[0],to_z)
-    got(2); got(5); add(po.at[x,1],[po.at[x,1],ro.at[5],ro.at[2]],SPLIT); go(17,po.at[x,1,:,lo],rp.at[1],to_z)
-    compute_own(right); go(8,pw.at[right,1],rw.at[2],to_right)
-    compute_own(left); go(9,pw.at[left,0],rw.at[3],to_left)
-    got(6); add(pw.at[right,0],[pw.at[right,0],rw.at[0]],feat); go(10,pw.at[right,0],rw.at[4],to_right)
-    got(7); add(pw.at[left,1],[pw.at[left,1],rw.at[1]],feat); go(11,pw.at[left,1],rw.at[5],to_left)
-    compute_own(x)
-    def final(h,a,b):
-        def low(j,_):
-            cc=pl.ds(pl.multiple_of(j*CC,CC),CC)
-            out_ref[h,:,cc]=(pw[x,h,:,cc].astype(f32)+rw[a,:,cc].astype(f32)+rw[b,:,cc].astype(f32)+rp[h,:,cc].astype(f32)).astype(bf); return 0
-        def high(j,_):
-            cc=pl.ds(pl.multiple_of(j*CC,CC),CC)
-            out_ref[h,:,cc]=(pw[x,h,:,cc].astype(f32)+rw[a,:,cc].astype(f32)+rw[b,:,cc].astype(f32)).astype(bf); return 0
-        lax.fori_loop(0,SPLIT//CC,low,0)
-        lax.fori_loop(SPLIT//CC,feat//CC,high,0)
-    got(9); got(10); got(16); final(0,4,3)
-    got(8); got(11); got(17); final(1,5,2)
-    for c in sent: c.wait_send()
-
-def project_scatter(d,wq,wk,wv):
-    seq,cols=d.shape; feat=wq.shape[0]; rows=seq//8; half=rows//2
-    any_=pl.BlockSpec(memory_space=pl.ANY); vm=pl.BlockSpec(memory_space=pltpu.VMEM)
-    bf=jnp.bfloat16
-    out=pl.pallas_call(scatter_kernel,
-        out_shape=jax.ShapeDtypeStruct((2,half,feat),bf),
-        in_specs=[vm]+[any_]*3,out_specs=vm,
-        scratch_shapes=[pltpu.VMEM((feat,cols),bf),pltpu.VMEM((4,2,half,feat),bf),pltpu.VMEM((4,2,half,feat),bf),
-            pltpu.VMEM((6,half,SPLIT),bf),pltpu.VMEM((6,half,feat),bf),pltpu.VMEM((4,2,half,feat-SPLIT),bf),pltpu.VMEM((2,half,SPLIT),bf),
-            pltpu.SemaphoreType.DMA((18,)),pltpu.SemaphoreType.DMA((18,)),pltpu.SemaphoreType.DMA((3,))],
-        compiler_params=pltpu.CompilerParams(collective_id=2,has_side_effects=True,vmem_limit_bytes=60*2**20),name="project_scatter",
-        cost_estimate=pl.CostEstimate(flops=2*seq*feat*cols,bytes_accessed=32*2**20,transcendentals=0),
-    )(d.reshape(8,rows,cols),wq,wk,wv)
-    return out.reshape(rows,feat)
-
-STAGES = ((("c",), (2,)), (("zl", "zh"), (2, 2)), (("y",), (4,)), (("x",), (4,)))
+
+CC = 512
+CUT = 5120
+PLANE = (("c", "zl", "zh"), (2, 2, 2))
+SHEET = (("y", "x"), (4, 4))
 
 
 def place(axes, sizes, index):
@@ -273,78 +176,316 @@
     return where
 
 
-def total_kernel(part_ref, out_ref, b0, b1, b2, b3, send, recv):
-    bufs = (b0, b1, b2, b3)
+def members(group):
+    axes, sizes = group
+    count = 1
+    me = jnp.int32(0)
+    for axis, size in zip(axes, sizes):
+        count *= size
+        me = me * size + lax.axis_index(axis)
+    others = [lax.rem(me + k, count) for k in range(1, count)]
+    return count, me, others, [place(axes, sizes, other) for other in others]
+
+
+def scatter_kernel(d_ref, n_ref, wq_ref, wk_ref, wv_ref, x_ref, inv_ref, gain_ref, out_ref, grad_ref, total_ref,
+                   w_s, part, ro, rw, rq, rp, n_s, dt_s, mine, g, ry, rz,
+                   send, recv, local, psend, precv, ysend, yrecv, nsem,
+                   plane, sheet, gsend, grecv):
+    x = lax.axis_index("x"); z = lax.axis_index("zh"); o = 1 - z
+    c = lax.axis_index("c"); y = lax.axis_index("y"); zl = lax.axis_index("zl")
+    right = lax.rem(x + 1, 4); left = lax.rem(x + 3, 4); far = lax.rem(x + 2, 4)
+    up = lax.rem(y + 1, 4); down = lax.rem(y + 3, 4); beyond = lax.rem(y + 2, 4)
+    to_right = {"x": right}; to_left = {"x": left}; to_z = {"zh": o}
+    to_up = {"y": up}; to_down = {"y": down}; to_core = {"c": 1 - c}; to_zl = {"zl": 1 - zl}
+    feat = part.shape[3]; half = part.shape[2]
+    lo = pl.ds(0, CUT); hi = pl.ds(CUT, feat - CUT)
+    wide = wq_ref.shape[1]; narrow = wk_ref.shape[1]
+    f32 = jnp.float32; bf = jnp.bfloat16
+    loads = [
+        pltpu.make_async_copy(wq_ref, w_s.at[:, pl.ds(0, wide)], local.at[0]),
+        pltpu.make_async_copy(wk_ref, w_s.at[:, pl.ds(wide, narrow)], local.at[1]),
+        pltpu.make_async_copy(wv_ref, w_s.at[:, pl.ds(wide + narrow, narrow)], local.at[2]),
+    ]
+    for copy in loads:
+        copy.start()
     bar = pltpu.get_barrier_semaphore()
-    plan = []
-    for axes, sizes in STAGES:
-        n = 1
-        me = jnp.int32(0)
-        for axis, size in zip(axes, sizes):
-            n *= size
-            me = me * size + lax.axis_index(axis)
-        others = [lax.rem(me + k, n) for k in range(1, n)]
-        plan.append((n, me, others, [place(axes, sizes, other) for other in others]))
-    count = 0
-    for n, me, others, devices in plan:
-        for device in devices:
-            pl.semaphore_signal(bar, inc=1, device_id=device, device_id_type=MESH)
-            count += 1
-    value = part_ref[...]
-    pl.semaphore_wait(bar, count)
-    for stage, (n, me, others, devices) in enumerate(plan):
-        buf = bufs[stage]
-        buf[me] = value
+    groups = (members(PLANE), members(SHEET))
+    everyone = groups[0][3] + groups[1][3]
+    for device in everyone:
+        pl.semaphore_signal(bar, inc=1, device_id=device, device_id_type=MESH)
+
+    blocks = g.shape[0]
+    width = g.shape[2]
+
+    def block_of(i):
+        j = lax.div(i, 2)
+        return 2 * lax.rem(y + 2 + jnp.where(j == 0, 0, lax.rem(j + 1, 3) + 1), 4) + lax.rem(i, 2)
+
+    def load(i):
+        owner = jnp.where(i < blocks, 1 - c, c)
+        k = block_of(lax.rem(i, blocks))
+        cols = pl.ds(pl.multiple_of((2 * k + owner) * width, width), width)
+        s = lax.rem(i, 2)
+        return pltpu.make_async_copy(n_ref.at[:, cols], n_s.at[s], nsem.at[s])
+
+    def pair(i):
+        k = block_of(i)
+        return pltpu.make_async_remote_copy(
+            src_ref=mine.at[lax.rem(i, 2)], dst_ref=g.at[k], send_sem=psend.at[i],
+            recv_sem=precv.at[i], device_id=to_core, device_id_type=MESH)
+
+    load(jnp.int32(0)).start()
+    dt_s[...] = jnp.concatenate([d_ref[s] for s in range(8)], axis=0).T
+
+    def product(i):
+        load(i).wait()
+        return jnp.dot(dt_s[...], n_s[lax.rem(i, 2)], preferred_element_type=f32)
+
+    def first(i, _):
+        load(i + 1).start()
+
+        @pl.when(i >= 2)
+        def _():
+            pair(i - 2).wait_send()
+
+        mine[lax.rem(i, 2)] = product(i).astype(bf)
+        pair(i).start()
+        return 0
+
+    def second(i, _):
+        @pl.when(i < blocks - 1)
+        def _():
+            load(i + blocks + 1).start()
+
+        value = product(i + blocks)
+        pair(i).wait_recv()
+        k = block_of(i)
+        g[k] = (value + g[k].astype(f32)).astype(bf)
+        return 0
+
+    place_of = (far, right, left, x)
+
+    def piece(rel, sz, j):
+        cc = pl.ds(pl.multiple_of(j * CC, CC), CC)
+        return cc, lax.dot_general(
+            d_ref[2 * place_of[rel] + sz], w_s[cc, :], (((1,), (1,)), ((), ())),
+            preferred_element_type=f32).reshape(2, half, CC)
+
+    def compute_other(rel):
+        def step(j, _):
+            cc, p = piece(rel, o, j)
+            part[rel, :, :, cc] = p.astype(bf)
+            return 0
+        lax.fori_loop(0, feat // CC, step, 0)
+
+    def compute_own(rel, slot):
+        def step(j, _):
+            cc, p = piece(rel, z, j)
+            part[slot, :, :, cc] = p.astype(bf)
+            return 0
+        lax.fori_loop(0, CUT // CC, step, 0)
+        got(12 + rel, rq.at[rel])
+
+        def step2(j, _):
+            cc, p = piece(rel, z, j)
+            qq = pl.ds(pl.multiple_of(j * CC - CUT, CC), CC)
+            part[slot, :, :, cc] = (p + rq[rel, :, :, qq].astype(f32)).astype(bf)
+            return 0
+        lax.fori_loop(CUT // CC, feat // CC, step2, 0)
+
+    sent = {}
+
+    def go(k, src, dst, dev):
+        copy = pltpu.make_async_remote_copy(
+            src_ref=src, dst_ref=dst, send_sem=send.at[k], recv_sem=recv.at[k],
+            device_id=dev, device_id_type=MESH)
+        copy.start()
+        sent[k] = copy
+
+    def got(k, ref):
+        pltpu.make_async_remote_copy(
+            src_ref=ref, dst_ref=ref, send_sem=send.at[k], recv_sem=recv.at[k],
+            device_id=to_z, device_id_type=MESH).wait_recv()
+
+    def zsend(rel):
+        go(12 + rel, part.at[rel, :, :, hi], rq.at[rel], to_z)
+
+    def free(*keys):
+        for k in keys:
+            sent.pop(k).wait_send()
+
+    def add(dst, terms, size):
+        def step(j, _):
+            cc = pl.ds(pl.multiple_of(j * CC, CC), CC)
+            acc = terms[0][:, cc].astype(f32)
+            for t in terms[1:]:
+                acc = acc + t[:, cc].astype(f32)
+            dst[:, cc] = acc.astype(bf)
+            return 0
+        lax.fori_loop(0, size // CC, step, 0)
+
+    ysent = []
+
+    def ygo(k, src, dst, dev):
+        copy = pltpu.make_async_remote_copy(
+            src_ref=src, dst_ref=dst, send_sem=ysend.at[k], recv_sem=yrecv.at[k],
+            device_id=dev, device_id_type=MESH)
+        copy.start()
+        ysent.append(copy)
+
+    def ygot(k, ref):
+        pltpu.make_async_remote_copy(
+            src_ref=ref, dst_ref=ref, send_sem=ysend.at[k], recv_sem=yrecv.at[k],
+            device_id=to_up, device_id_type=MESH).wait_recv()
+
+    for copy in loads:
+        copy.wait()
+    compute_other(0)
+    pl.semaphore_wait(bar, len(everyone))
+    go(0, part.at[0, 0, :, lo], ro.at[0], to_right); go(1, part.at[0, 1, :, lo], ro.at[1], to_left); zsend(0)
+    compute_other(1); go(2, part.at[1, 1, :, lo], ro.at[2], to_right); zsend(1)
+    compute_other(2); go(3, part.at[2, 0, :, lo], ro.at[3], to_left); zsend(2)
+    compute_other(3); zsend(3)
+    got(0, ro.at[0]); add(part.at[1, 0], [part.at[1, 0], ro.at[0]], CUT); go(4, part.at[1, 0, :, lo], ro.at[4], to_right)
+    got(1, ro.at[1]); add(part.at[2, 1], [part.at[2, 1], ro.at[1]], CUT); go(5, part.at[2, 1, :, lo], ro.at[5], to_left)
+    lax.fori_loop(0, blocks, first, 0)
+    compute_own(0, 4)
+    go(6, part.at[4, 0], rw.at[0], to_right); go(7, part.at[4, 1], rw.at[1], to_left)
+    lax.fori_loop(0, 2, second, 0)
+    ygo(0, g.at[2 * beyond], ry.at[0], to_up); ygo(1, g.at[2 * beyond + 1], ry.at[1], to_down)
+    lax.fori_loop(2, 6, second, 0)
+    ygo(2, g.at[2 * up + 1], ry.at[2], to_up); ygo(3, g.at[2 * down], ry.at[3], to_down)
+    lax.fori_loop(6, 8, second, 0)
+    got(3, ro.at[3]); got(4, ro.at[4]); add(part.at[3, 0], [part.at[3, 0], ro.at[4], ro.at[3]], CUT); go(16, part.at[3, 0, :, lo], rp.at[0], to_z)
+    got(2, ro.at[2]); got(5, ro.at[5]); add(part.at[3, 1], [part.at[3, 1], ro.at[5], ro.at[2]], CUT); go(17, part.at[3, 1, :, lo], rp.at[1], to_z)
+    compute_own(1, 5); go(8, part.at[5, 1], rw.at[2], to_right)
+    ygot(0, ry.at[0]); add(g.at[2 * up], [g.at[2 * up], ry.at[0]], width); ygo(4, g.at[2 * up], ry.at[4], to_up)
+    ygot(1, ry.at[1]); add(g.at[2 * down + 1], [g.at[2 * down + 1], ry.at[1]], width); ygo(5, g.at[2 * down + 1], ry.at[5], to_down)
+    free(0, 1, 12)
+    compute_own(2, 0); go(9, part.at[0, 0], rw.at[3], to_left)
+    got(6, rw.at[0]); add(part.at[5, 0], [part.at[5, 0], rw.at[0]], feat); go(10, part.at[5, 0], rw.at[4], to_right)
+    got(7, rw.at[1]); add(part.at[0, 1], [part.at[0, 1], rw.at[1]], feat); go(11, part.at[0, 1], rw.at[5], to_left)
+    free(2, 4, 13)
+    free(3, 5, 14)
+    x_load = pltpu.make_async_copy(x_ref, part.at[2], local.at[3])
+    x_load.start()
+    compute_own(3, 1)
+    ygot(3, ry.at[3]); ygot(4, ry.at[4]); add(g.at[2 * y], [g.at[2 * y], ry.at[4], ry.at[3]], width)
+    ygot(2, ry.at[2]); ygot(5, ry.at[5]); add(g.at[2 * y + 1], [g.at[2 * y + 1], ry.at[5], ry.at[2]], width)
+    ygo(6, g.at[2 * y + 1 - zl], rz, to_zl)
+
+    def final(h, a, b):
+        inv = inv_ref[h]
+
+        def step(with_z, j, acc):
+            cc = pl.ds(pl.multiple_of(j * CC, CC), CC)
+            nd = (part[1, h, :, cc].astype(f32) + rw[a, :, cc].astype(f32) + rw[b, :, cc].astype(f32))
+            if with_z:
+                nd = nd + rp[h, :, cc].astype(f32)
+            part[1, h, :, cc] = nd.astype(bf)
+            nd = nd * (part[2, h, :, cc].astype(f32) * inv)
+            where = (me_plane, pl.ds(lax.div(j, 2), 1), pl.ds(pl.multiple_of(lax.rem(j, 2) * CC, CC), CC))
+            term = jnp.sum(nd, axis=0, keepdims=True)
+            if h:
+                term = term + plane[where]
+            plane[where] = term
+            nd = nd * gain_ref[0:1, cc]
+            for q in range(CC // 128):
+                acc = acc + nd[:, q * 128:(q + 1) * 128]
+            return acc
+
+        acc = jnp.zeros((half, 128), f32)
+        acc = lax.fori_loop(0, CUT // CC, lambda j, v: step(True, j, v), acc)
+        acc = lax.fori_loop(CUT // CC, feat // CC, lambda j, v: step(False, j, v), acc)
+        return jnp.sum(acc, axis=1, keepdims=True) * (1.0 / feat)
+
+    def input_gradient(h, mean):
+        inv = inv_ref[h]
+
+        def step(j, _):
+            cc = pl.ds(pl.multiple_of(j * CC, CC), CC)
+            nd = part[1, h, :, cc].astype(f32)
+            part[1, h, :, cc] = (inv * (nd * gain_ref[0:1, cc] - part[2, h, :, cc].astype(f32) * inv * mean)).astype(bf)
+            return 0
+        lax.fori_loop(0, feat // CC, step, 0)
+
+    def share(stage, buf):
+        count, me, others, devices = groups[stage]
         copies = []
         for k, device in enumerate(devices):
             copy = pltpu.make_async_remote_copy(
-                src_ref=buf.at[me],
-                dst_ref=buf.at[me],
-                send_sem=send.at[stage, k],
-                recv_sem=recv.at[stage, me],
-                device_id=device,
-                device_id_type=MESH,
-            )
+                src_ref=buf.at[me], dst_ref=buf.at[me], send_sem=gsend.at[stage, k],
+                recv_sem=grecv.at[stage, me], device_id=device, device_id_type=MESH)
             copy.start()
             copies.append(copy)
+        return copies
+
+    def gather_sum(stage, buf, copies):
+        count, me, others, devices = groups[stage]
         for k, other in enumerate(others):
             pltpu.make_async_remote_copy(
-                src_ref=buf.at[other],
-                dst_ref=buf.at[other],
-                send_sem=send.at[stage, k],
-                recv_sem=recv.at[stage, other],
-                device_id=devices[k],
-                device_id_type=MESH,
-            ).wait_recv()
+                src_ref=buf.at[other], dst_ref=buf.at[other], send_sem=gsend.at[stage, k],
+                recv_sem=grecv.at[stage, other], device_id=devices[k], device_id_type=MESH).wait_recv()
         value = buf[0]
-        for k in range(1, n):
+        for k in range(1, count):
             value = value + buf[k]
         for copy in copies:
             copy.wait_send()
-    out_ref[...] = value
-
-
-def total_over_devices(part):
-    vm = pl.BlockSpec(memory_space=pltpu.VMEM)
-    shape = (part.shape[0] // 128, 128)
-    out = pl.pallas_call(
-        total_kernel,
-        out_shape=jax.ShapeDtypeStruct(shape, jnp.float32),
-        in_specs=[vm],
-        out_specs=vm,
+        return value
+
+    me_plane, me_sheet = groups[0][1], groups[1][1]
+    x_load.wait()
+    got(9, rw.at[3]); got(10, rw.at[4]); got(16, rp.at[0]); mean0 = final(0, 4, 3)
+    got(8, rw.at[2]); got(11, rw.at[5]); got(17, rp.at[1]); mean1 = final(1, 5, 2)
+    copies = share(0, plane)
+    input_gradient(0, mean0)
+    store0 = pltpu.make_async_copy(part.at[1, 0], out_ref.at[0], local.at[0])
+    store0.start()
+    value = gather_sum(0, plane, copies)
+    sheet[me_sheet] = value
+    copies = share(1, sheet)
+    input_gradient(1, mean1)
+    store1 = pltpu.make_async_copy(part.at[1, 1], out_ref.at[1], local.at[1])
+    store1.start()
+    total_ref[...] = gather_sum(1, sheet, copies)
+    ygot(6, rz); add(grad_ref, [g.at[2 * y + zl], rz], width)
+    store0.wait()
+    store1.wait()
+    for copy in ysent:
+        copy.wait_send()
+    for i in (blocks - 2, blocks - 1):
+        pair(jnp.int32(i)).wait_send()
+    free(*list(sent))
+
+
+def project_scatter(d, normed, wq, wk, wv, x, inverse, gain):
+    seq, cols = d.shape; feat = wq.shape[0]; rows = seq // 8; half = rows // 2
+    width = feat // 16
+    any_ = pl.BlockSpec(memory_space=pl.ANY); vm = pl.BlockSpec(memory_space=pltpu.VMEM)
+    bf = jnp.bfloat16
+    dma = pltpu.SemaphoreType.DMA
+    out, grad, total = pl.pallas_call(
+        scatter_kernel,
+        out_shape=(jax.ShapeDtypeStruct((2, half, feat), bf), jax.ShapeDtypeStruct((cols, width), bf),
+                   jax.ShapeDtypeStruct((8, feat // 8), jnp.float32)),
+        in_specs=[vm] + [any_] * 5 + [vm] * 2, out_specs=(any_, vm, vm),
         scratch_shapes=[
-            pltpu.VMEM((2,) + shape, jnp.float32),
-            pltpu.VMEM((4,) + shape, jnp.float32),
-            pltpu.VMEM((4,) + shape, jnp.float32),
-            pltpu.VMEM((4,) + shape, jnp.float32),
-            pltpu.SemaphoreType.DMA((4, 4)),
-            pltpu.SemaphoreType.DMA((4, 4)),
+            pltpu.VMEM((feat, cols), bf), pltpu.VMEM((6, 2, half, feat), bf),
+            pltpu.VMEM((6, half, CUT), bf), pltpu.VMEM((6, half, feat), bf),
+            pltpu.VMEM((4, 2, half, feat - CUT), bf), pltpu.VMEM((2, half, CUT), bf),
+            pltpu.VMEM((2, seq, width), bf), pltpu.VMEM((cols, seq), bf),
+            pltpu.VMEM((2, cols, width), bf), pltpu.VMEM((8, cols, width), bf),
+            pltpu.VMEM((6, cols, width), bf), pltpu.VMEM((cols, width), bf),
+            dma((18,)), dma((18,)), dma((4,)), dma((8,)), dma((8,)), dma((7,)), dma((7,)), dma((2,)),
+            pltpu.VMEM((8, 8, feat // 8), jnp.float32), pltpu.VMEM((16, 8, feat // 8), jnp.float32),
+            dma((2, 16)), dma((2, 16)),
         ],
-        compiler_params=pltpu.CompilerParams(collective_id=3, has_side_effects=True),
-        name="total",
-        cost_estimate=pl.CostEstimate(flops=10**9, bytes_accessed=10**6, transcendentals=0),
-    )(part.reshape(shape))
-    return out.reshape(part.shape)
+        compiler_params=pltpu.CompilerParams(collective_id=2, has_side_effects=True, vmem_limit_bytes=63 * 2**20),
+        name="project_scatter",
+        cost_estimate=pl.CostEstimate(flops=4 * seq * feat * cols, bytes_accessed=48 * 2**20, transcendentals=0),
+    )(d.reshape(8, rows, cols), normed, wq, wk, wv,
+      x.reshape(2, half, feat), inverse.reshape(2, half, 1), gain.reshape(1, feat))
+    return out.reshape(rows, feat), grad, total.reshape(feat)
 
 
 def rope_tables(segment_row):
@@ -366,18 +507,10 @@
     qkv, normed = gather_project(own, w_query, w_key, w_value)
     cosine, sine = rope_tables(segment_row)
     attended, heads_d = attention(qkv, attended_grad, cosine, sine, segment_row)
-    products = lax.dot_general(
-        normed, heads_d, (((0,), (0,)), ((), ())), preferred_element_type=jnp.float32
-    ).astype(jnp.bfloat16)
-    heads_d, products = lax.optimization_barrier((heads_d, products))
-    merged = lax.psum_scatter(products, DP, scatter_dimension=0, tiled=True).astype(jnp.float32)
-    normed_d = project_scatter(heads_d, w_query, w_key, w_value).astype(jnp.float32)
-    x_hat = x_tokens.astype(jnp.float32) * inverse
-    scaled_d = normed_d * norm_gain
-    input_grad = (
-        inverse * (scaled_d - x_hat * jnp.mean(scaled_d * x_hat, axis=1, keepdims=True))
-    ).astype(jnp.bfloat16)
-    gain_grad = total_over_devices(jnp.sum(normed_d * x_hat, axis=0))
+    input_grad, merged, gain_grad = project_scatter(
+        heads_d, normed, w_query, w_key, w_value, x_tokens, inverse, norm_gain
+    )
+    merged = merged.T.astype(jnp.float32)
     query_cols, key_cols = w_query.shape[1], w_key.shape[1]
     return (
         attended,

time: 444 us -> 298 us (0.67)
  Pallas kernels: 385 us -> 279 us
  matrix products: 20.2 us -> 0 us
  between operations: 14.1 us -> 0.74 us
  other arithmetic: 16.4 us -> 8.36 us
    pallas_call x2 -> x1, Pallas kernels: 249 us -> 143 us  [project_scatter(): pl.pallas_call(scatter_kernel, out_shape=(jax.ShapeDtypeStruct((2, half,...]
    dot_general x1 -> x0, matrix products: 20.2 us -> none  [body(): lax.dot_general(normed, heads_d, (((0,), (0,)), ((), ())), preferred_elem...]
    unnamed x7 -> x13, local copies, waits for them, and re-layouts: 0.63 us -> 6.72 us
  transfers between devices with their start and end apart: 1 -> 0, of which waited for: 0 -> 0; matrix products, arithmetic and copies ran while one was open for 2% -> 0% of each run, Pallas kernels for 56% -> 0%
where the time goes in v3:
time: 298 us; the launch traced here: 297 us
  Pallas kernels  279 us (94%)
  local copies, waits for them, and re-layouts  8.68 us (3%)
  other arithmetic  8.36 us (3%)
    pallas_call x1, Pallas kernels, project_scatter(): pl.pallas_call(scatter_kernel, out_shape=(jax.ShapeDtypeStruct((2, half,...  143 us
    pallas_call x1, Pallas kernels, gather_project(): pl.pallas_call(gather_kernel, out_shape=(jax.ShapeDtypeStruct((8 * rows,...  117 us
    pallas_call x1, Pallas kernels, attention(): pl.pallas_call(attention_kernel, out_shape=(jax.ShapeDtypeStruct(go.shape...  19.4 us
    unnamed x13, local copies, waits for them, and re-layouts  6.72 us

profile of v3, /device:TPU:1, one launch (start us, length us, event | category | flops | bytes accessed | tf_op | source)
XLA Modules:
  0.0 297.2 jit_solution(1794833617709391003)
XLA Ops:
  0.6 0.0 copy-start
  0.6 1.4 convert_reduce_fusion
  2.1 0.0 copy-start.2
  2.1 1.9 fusion.3
  4.0 1.3 pad_maximum_fusion
  5.3 0.0 copy-done
  5.3 0.5 fusion
  5.8 0.0 copy-done.2
  5.8 1.9 fusion.2
  7.7 0.0 copy-start.1
  7.7 117.0 %gather_project.1 = (f32[1024,768]{1,0:T(8,128)}, bf16[8,2,64,8192]{3,2,1,0:T(8,128)(2,1)}) custom-call(bf16[2,64,8192]{2,1,0:T(8,128)(2,1)} %bitcast.16, bf16[8192,512]{1,0:T(8,128)(2,1)} %wq_ref.3, bf16[8192,128]{1,0:T(8,128)(2,1)} %wk_ref.3, bf16[8192,128]{1,0:T(8,128)(2,1)} %wv_ref.3), custom_call_target="tpu_custom_call" | custom-call | flops 12884901888 | bytes 50331648 | tf_op jit(solution)/shard_map/gather_project/pallas_call | solution.py:96
  124.7 0.0 copy-done.1
  124.8 1.0 copy.22.segc_ref
  125.8 19.4 %attention.1 = (bf16[1024,512]{1,0:T(8,128)(2,1)}, bf16[1024,768]{1,0:T(8,128)(2,1)}) custom-call(f32[1024,768]{1,0:T(8,128)} %get-tuple-element.13.qkv_ref, bf16[1024,512]{1,0:T(8,128)(2,1)} %go_ref.1, f32[1024,128]{1,0:T(8,128)} %get-tuple-element.43.cos_ref, f32[1024,128]{1,0:T(8,128)} %get-tuple-element.44.sin_ref, s32[1,1024]{1,0:T(1,128)} %segr_ref.1, ...), custom_call_target="tpu_custom_call" | custom-call | flops 3221225472 | bytes 12582912 | tf_op jit(solution)/shard_map/attention/pallas_call | solution.py:157
  145.1 0.8 rsqrt.20.inv_ref
  146.0 143.0 %project_scatter.1 = (bf16[2,64,8192]{2,1,0:T(8,128)(2,1)}, bf16[768,512]{1,0:T(8,128)(2,1)}, f32[8,1024]{1,0:T(8,128)}) custom-call(bf16[8,128,768]{2,1,0:T(8,128)(2,1)} %bitcast.23, bf16[1024,8192]{1,0:T(8,128)(2,1)} %bitcast.22, bf16[8192,512]{1,0:T(8,128)(2,1)} %wq_ref.3, bf16[8192,128]{1,0:T(8,128)(2,1)} %wk_ref.3, bf16[8192,128]{1,0:T(8,128)(2,1)} %wv_ref.3, ...), custom_call_target="tpu_custom_call" | custom-call | flops 25769803776 | bytes 50331648 | tf_op jit(solution)/shard_map/project_scatter/pallas_call | solution.py:467
  289.0 1.3 convert_bitcast_fusion
  290.3 0.0 copy-start.3
  290.4 0.8 copy.25
  291.2 0.8 copy.26
  292.1 0.1 slice.12
  292.1 1.3 copy.24
  293.4 0.0 copy-done.3
  293.4 0.6 copy.29
  294.1 3.1 %copy.31 = bf16[128,8192]{1,0:T(8,128)(2,1)} copy(bf16[128,8192]{1,0:T(8,128)(2,1)} %bitcast.15) | data formatting | bytes 4194304
  (4 shorter events, 0.1 us)
Async XLA Ops:
  0.6 4.7 %copy-start = (bf16[128,8192]{1,0:T(8,128)(2,1)S(1)}, bf16[128,8192]{1,0:T(8,128)(2,1)}, u32[]{:S(2)}) copy-start(bf16[128,8192]{1,0:T(8,128)(2,1)} %param.7) | copy-start | bytes 6291460
  2.1 3.7 %copy-start.2 = (f32[8192]{0:T(1024)S(1)}, f32[8192]{0:T(1024)}, u32[]{:S(2)}) copy-start(f32[8192]{0:T(1024)} %param.10) | copy-start | bytes 98308
  7.7 117.0 %copy-start.1 = (s32[1,1024]{1,0:T(1,128)S(1)}, s32[1,1024]{1,0:T(1,128)}, u32[]{:S(2)}) copy-start(s32[1,1024]{1,0:T(1,128)} %segr_ref.1) | copy-start | bytes 12292
  290.3 3.1 %copy-start.3 = (f32[8,1024]{1,0:T(8,128)S(1)}, f32[8,1024]{1,0:T(8,128)}, u32[]{:S(2)}) copy-start(f32[8,1024]{1,0:T(8,128)} %get-tuple-element.18) | copy-start | bytes 98308

commit v4 on v3

--- a/solution.py
+++ b/solution.py
@@ -190,7 +190,7 @@
 def scatter_kernel(d_ref, n_ref, wq_ref, wk_ref, wv_ref, x_ref, inv_ref, gain_ref, out_ref, grad_ref, total_ref,
                    w_s, part, ro, rw, rq, rp, n_s, dt_s, mine, g, ry, rz,
                    send, recv, local, psend, precv, ysend, yrecv, nsem,
-                   plane, sheet, gsend, grecv):
+                   plane, sheet, gsend, grecv, wsem):
     x = lax.axis_index("x"); z = lax.axis_index("zh"); o = 1 - z
     c = lax.axis_index("c"); y = lax.axis_index("y"); zl = lax.axis_index("zl")
     right = lax.rem(x + 1, 4); left = lax.rem(x + 3, 4); far = lax.rem(x + 2, 4)
@@ -201,13 +201,20 @@
     lo = pl.ds(0, CUT); hi = pl.ds(CUT, feat - CUT)
     wide = wq_ref.shape[1]; narrow = wk_ref.shape[1]
     f32 = jnp.float32; bf = jnp.bfloat16
-    loads = [
-        pltpu.make_async_copy(wq_ref, w_s.at[:, pl.ds(0, wide)], local.at[0]),
-        pltpu.make_async_copy(wk_ref, w_s.at[:, pl.ds(wide, narrow)], local.at[1]),
-        pltpu.make_async_copy(wv_ref, w_s.at[:, pl.ds(wide + narrow, narrow)], local.at[2]),
-    ]
-    for copy in loads:
-        copy.start()
+    def w_loads(j):
+        rr = pl.ds(pl.multiple_of(j * CC, CC), CC)
+        return (
+            pltpu.make_async_copy(wq_ref.at[rr], w_s.at[rr, pl.ds(0, wide)], wsem.at[0, j]),
+            pltpu.make_async_copy(wk_ref.at[rr], w_s.at[rr, pl.ds(wide, narrow)], wsem.at[1, j]),
+            pltpu.make_async_copy(wv_ref.at[rr], w_s.at[rr, pl.ds(wide + narrow, narrow)], wsem.at[2, j]),
+        )
+
+    def w_start(j, _):
+        for copy in w_loads(j):
+            copy.start()
+        return 0
+
+    lax.fori_loop(0, feat // CC, w_start, 0)
     bar = pltpu.get_barrier_semaphore()
     groups = (members(PLANE), members(SHEET))
     everyone = groups[0][3] + groups[1][3]
@@ -273,6 +280,9 @@
 
     def compute_other(rel):
         def step(j, _):
+            if rel == 0:
+                for copy in w_loads(j):
+                    copy.wait()
             cc, p = piece(rel, o, j)
             part[rel, :, :, cc] = p.astype(bf)
             return 0
@@ -338,8 +348,6 @@
             src_ref=ref, dst_ref=ref, send_sem=ysend.at[k], recv_sem=yrecv.at[k],
             device_id=to_up, device_id_type=MESH).wait_recv()
 
-    for copy in loads:
-        copy.wait()
     compute_other(0)
     pl.semaphore_wait(bar, len(everyone))
     go(0, part.at[0, 0, :, lo], ro.at[0], to_right); go(1, part.at[0, 1, :, lo], ro.at[1], to_left); zsend(0)
@@ -478,7 +486,7 @@
             pltpu.VMEM((6, cols, width), bf), pltpu.VMEM((cols, width), bf),
             dma((18,)), dma((18,)), dma((4,)), dma((8,)), dma((8,)), dma((7,)), dma((7,)), dma((2,)),
             pltpu.VMEM((8, 8, feat // 8), jnp.float32), pltpu.VMEM((16, 8, feat // 8), jnp.float32),
-            dma((2, 16)), dma((2, 16)),
+            dma((2, 16)), dma((2, 16)), dma((3, feat // CC)),
         ],
         compiler_params=pltpu.CompilerParams(collective_id=2, has_side_effects=True, vmem_limit_bytes=63 * 2**20),
         name="project_scatter",

time: 298 us -> 295 us (0.990)
  Pallas kernels: 279 us -> 276 us
    pallas_call x1, Pallas kernels: 143 us -> 140 us  [project_scatter(): pl.pallas_call(scatter_kernel, out_shape=(jax.ShapeDtypeStruct((2, half,...]
where the time goes in v4:
time: 295 us; the launch traced here: 294 us
  Pallas kernels  276 us (94%)
  local copies, waits for them, and re-layouts  8.68 us (3%)
  other arithmetic  8.36 us (3%)
    pallas_call x1, Pallas kernels, project_scatter(): pl.pallas_call(scatter_kernel, out_shape=(jax.ShapeDtypeStruct((2, half,...  140 us
    pallas_call x1, Pallas kernels, gather_project(): pl.pallas_call(gather_kernel, out_shape=(jax.ShapeDtypeStruct((8 * rows,...  117 us
    pallas_call x1, Pallas kernels, attention(): pl.pallas_call(attention_kernel, out_shape=(jax.ShapeDtypeStruct(go.shape...  19.4 us
    unnamed x13, local copies, waits for them, and re-layouts  6.72 us

profile of v4, /device:TPU:1, one launch (start us, length us, event | category | flops | bytes accessed | tf_op | source)
XLA Modules:
  0.0 294.1 jit_solution(8100563032568118360)
XLA Ops:
  0.6 0.0 copy-start
  0.6 1.4 convert_reduce_fusion
  2.1 0.0 copy-start.2
  2.1 1.9 fusion.3
  4.0 1.3 pad_maximum_fusion
  5.3 0.0 copy-done
  5.3 0.5 fusion
  5.8 0.0 copy-done.2
  5.8 1.9 fusion.2
  7.7 0.0 copy-start.1
  7.7 117.0 %gather_project.1 = (f32[1024,768]{1,0:T(8,128)}, bf16[8,2,64,8192]{3,2,1,0:T(8,128)(2,1)}) custom-call(bf16[2,64,8192]{2,1,0:T(8,128)(2,1)} %bitcast.16, bf16[8192,512]{1,0:T(8,128)(2,1)} %wq_ref.3, bf16[8192,128]{1,0:T(8,128)(2,1)} %wk_ref.3, bf16[8192,128]{1,0:T(8,128)(2,1)} %wv_ref.3), custom_call_target="tpu_custom_call" | custom-call | flops 12884901888 | bytes 50331648 | tf_op jit(solution)/shard_map/gather_project/pallas_call | solution.py:96
  124.7 0.0 copy-done.1
  124.8 1.0 copy.22.segc_ref
  125.8 19.4 %attention.1 = (bf16[1024,512]{1,0:T(8,128)(2,1)}, bf16[1024,768]{1,0:T(8,128)(2,1)}) custom-call(f32[1024,768]{1,0:T(8,128)} %get-tuple-element.13.qkv_ref, bf16[1024,512]{1,0:T(8,128)(2,1)} %go_ref.1, f32[1024,128]{1,0:T(8,128)} %get-tuple-element.43.cos_ref, f32[1024,128]{1,0:T(8,128)} %get-tuple-element.44.sin_ref, s32[1,1024]{1,0:T(1,128)} %segr_ref.1, ...), custom_call_target="tpu_custom_call" | custom-call | flops 3221225472 | bytes 12582912 | tf_op jit(solution)/shard_map/attention/pallas_call | solution.py:157
  145.1 0.8 rsqrt.20.inv_ref
  146.0 140.0 %project_scatter.1 = (bf16[2,64,8192]{2,1,0:T(8,128)(2,1)}, bf16[768,512]{1,0:T(8,128)(2,1)}, f32[8,1024]{1,0:T(8,128)}) custom-call(bf16[8,128,768]{2,1,0:T(8,128)(2,1)} %bitcast.23, bf16[1024,8192]{1,0:T(8,128)(2,1)} %bitcast.22, bf16[8192,512]{1,0:T(8,128)(2,1)} %wq_ref.3, bf16[8192,128]{1,0:T(8,128)(2,1)} %wk_ref.3, bf16[8192,128]{1,0:T(8,128)(2,1)} %wv_ref.3, ...), custom_call_target="tpu_custom_call" | custom-call | flops 25769803776 | bytes 50331648 | tf_op jit(solution)/shard_map/project_scatter/pallas_call | solution.py:475
  285.9 1.3 convert_bitcast_fusion
  287.3 0.0 copy-start.3
  287.3 0.8 copy.25
  288.2 0.8 copy.26
  289.0 0.1 slice.12
  289.1 1.3 copy.24
  290.4 0.0 copy-done.3
  290.4 0.6 copy.29
  291.0 3.1 %copy.31 = bf16[128,8192]{1,0:T(8,128)(2,1)} copy(bf16[128,8192]{1,0:T(8,128)(2,1)} %bitcast.15) | data formatting | bytes 4194304
  (4 shorter events, 0.1 us)
Async XLA Ops:
  0.6 4.7 %copy-start = (bf16[128,8192]{1,0:T(8,128)(2,1)S(1)}, bf16[128,8192]{1,0:T(8,128)(2,1)}, u32[]{:S(2)}) copy-start(bf16[128,8192]{1,0:T(8,128)(2,1)} %param.7) | copy-start | bytes 6291460
  2.1 3.7 %copy-start.2 = (f32[8192]{0:T(1024)S(1)}, f32[8192]{0:T(1024)}, u32[]{:S(2)}) copy-start(f32[8192]{0:T(1024)} %param.10) | copy-start | bytes 98308
  7.7 117.0 %copy-start.1 = (s32[1,1024]{1,0:T(1,128)S(1)}, s32[1,1024]{1,0:T(1,128)}, u32[]{:S(2)}) copy-start(s32[1,1024]{1,0:T(1,128)} %segr_ref.1) | copy-start | bytes 12292
  287.3 3.1 %copy-start.3 = (f32[8,1024]{1,0:T(8,128)S(1)}, f32[8,1024]{1,0:T(8,128)}, u32[]{:S(2)}) copy-start(f32[8,1024]{1,0:T(8,128)} %get-tuple-element.18) | copy-start | bytes 98308
